TPU v7x, 256 devices: a whole 4x4x8 slice. The times are simulated.
256 devices in a mesh: latent: 64 (over y, x_hi, z), dp: 4 (over x_lo, core).
Axes of the slice: x: 4 (x_hi: 2, x_lo: 2; x = x_hi * 2 + x_lo), y: 4, z: 8, core: 2. Of those that a mesh axis runs over, the one named last changes fastest.
Arguments:
- codes_val: bfloat16 [256, 64], replicated, may hold values from 0.049804688 to 4
- codes_idx: int32 [256, 64], replicated, may hold values from 0 to 98303, as said below
- target: bfloat16 [256, 6144], P(('latent', 'dp')), may hold values from -6 to 6
- dec_weight: bfloat16 [98304, 6144], P(('latent', 'dp')), may hold values from -0.75 to 0.75
- dec_bias: float32 [6144], replicated, may hold values from -3 to 3
- basis: float32 [6144, 256], P('dp'), may hold values from -0.375 to 0.375
- first_mom: float32 [98304, 256], P(('latent', 'dp')), may hold values from -3 to 3
- second_mom: float32 [98304, 256], P(('latent', 'dp')), may hold values from 0.02 to 0.2
Outputs:
- update: bfloat16 [98304, 6144], P(('latent', 'dp'))
- first_new: float32 [98304, 256], P(('latent', 'dp'))
- second_new: float32 [98304, 256], P(('latent', 'dp'))
- code_grad: float32 [256, 64], P(('latent', 'dp'))
Inputs may be any that keep to these rules, and one draw needn't show every extreme that they name: `codes_idx`: A token's 64 latent numbers are distinct. Number the devices in the order latent then dp; device s holds latents s * 384 to (s + 1) * 384 - 1 and the token rows of its block of 256 / (64 * 4). Of the active pairs of one device's token rows, at most 1 fall in one device's latents, and in every such block some device's latents receive exactly 1.
All inputs are finite; a program needn't handle non-finite values.
Results may differ from a plain program's by a relative error of at most 0.0038.
Values may be sent and summed in bfloat16 or wider, within the bound.
No kernel may reach another device: no remote copies, remote signals or barrier semaphores. Data moves between devices by JAX's collectives and lax.ppermute only.
A program may use at most 128 MiB of HBM per device.

v0:
```python
import math

import jax
import jax.numpy as jnp
from jax import lax
from jax.sharding import Mesh
from jax.sharding import PartitionSpec as P

DP = ("dp_0", "dp_1")
LATENT_DP = ("latent", "dp_0", "dp_1")


beta_one = 0.9
beta_two = 0.999
epsilon = 1e-08
first_fix = 1.0 - math.exp(100.0 * math.log(0.9))
second_fix = 1.0 - math.exp(100.0 * math.log(0.999))


def in_order(pieces, dim):
    pieces = jnp.moveaxis(pieces, 0, dim)
    lengths = pieces.shape
    return pieces.reshape(*lengths[:dim], lengths[dim] * lengths[dim + 1], *lengths[dim + 2 :])


def gather_in_order(array, axes, turns):
    pieces = array
    for k in turns:
        pieces = lax.all_gather(pieces, axes[k])
    done = turns[::-1]
    back = [done.index(k) for k in range(len(axes))]
    pieces = pieces.transpose(*back, *range(len(axes), pieces.ndim))
    return pieces.reshape(-1, *array.shape)


def gathered_by_axis(array, axes, turns, dim):
    return in_order(gather_in_order(array, axes, turns), dim)


def split_up(array, dim, peers):
    before, after = (array.shape[:dim], array.shape[dim + 1 :])
    return jnp.moveaxis(array.reshape(*before, peers, -1, *after), dim, 0)


def joined_exchange(array, axis, axes, splits, concats):
    sizes = [lax.axis_size(a) for a in axes]
    pieces = split_up(array, splits[0], sizes[0])
    pieces = jnp.moveaxis(split_up(pieces, splits[1] + 1, sizes[1]), 0, 1)
    inside = pieces.shape[2:]
    pieces = pieces.reshape(-1, *inside)
    pieces = lax.all_to_all(pieces, axis, split_axis=0, concat_axis=0, tiled=True)
    pieces = in_order(pieces.reshape(*sizes, *inside), concats[0] + 1)
    return in_order(pieces, concats[1])


def spread_codes(values, indices, start, width):
    local = indices - start
    inside = (local >= 0) & (local < width)
    slot = jnp.where(inside, local, width)
    rows = indices.shape[0]
    topk = indices.shape[1]
    columns = jnp.arange(width, dtype=jnp.int32)

    def spread_one_block(pair):
        block_val, block_slot = pair
        hit = block_slot[:, :, None] == columns[None, None, :]
        return jnp.sum(
            jnp.where(hit, block_val.astype(jnp.float32)[:, :, None], jnp.float32(0.0)), axis=1
        )

    dense = lax.map(
        spread_one_block,
        (values.reshape(rows // rows, rows, topk), slot.reshape(rows // rows, rows, topk)),
    )
    dense = dense.reshape(rows, width)
    return (dense.astype(jnp.bfloat16), inside, jnp.where(inside, local, 0))


def pick_columns(matrix, slot):
    rows = slot.shape[0]
    topk = slot.shape[1]
    width = matrix.shape[1]
    columns = jnp.arange(width, dtype=jnp.int32)

    def pick_one_block(pair):
        block_mat, block_slot = pair
        hit = block_slot[:, :, None] == columns[None, None, :]
        return jnp.sum(jnp.where(hit, block_mat[:, None, :], jnp.float32(0.0)), axis=2)

    picked = lax.map(
        pick_one_block,
        (matrix.reshape(rows // rows, rows, width), slot.reshape(rows // rows, rows, topk)),
    )
    return picked.reshape(rows, topk)


def adam_rows(proj, first_mom, second_mom):
    first_out = beta_one * first_mom + (1.0 - beta_one) * proj
    second_out = beta_two * second_mom + (1.0 - beta_two) * proj * proj
    normed = first_out / first_fix / (jnp.sqrt(second_out / second_fix) + epsilon)
    return (first_out, second_out, normed)


def shards(codes_val, codes_idx, target, dec_weight, dec_bias, basis, first_mom, second_mom):
    width = dec_weight.shape[0]
    model = dec_weight.shape[1]
    n_dp = lax.axis_size(DP)
    n_lat = lax.axis_size("latent")
    n_dev = n_lat * n_dp
    device = lax.axis_index("latent") * n_dp + lax.axis_index(DP)
    start = device * width
    whole_basis = gathered_by_axis(basis, DP, (0, 1), 0)
    tokens = codes_idx.shape[0]
    topk = codes_idx.shape[1]
    share = target.shape[0]
    cap = max(1, 2 * tokens * topk // (n_dev * n_dev))
    pairs = share * topk
    slots = n_dev * cap
    mine = codes_idx // width == device
    rank = jnp.cumsum(mine.astype(jnp.int32), axis=1) - 1
    owners = jnp.arange(n_dev, dtype=jnp.int32)[:, None]
    place = jnp.where(mine, owners * cap + rank, slots).reshape(-1)
    local = (codes_idx - start).reshape(-1)
    table_lat = jnp.zeros((slots,), jnp.int32).at[place].set(local, mode="drop")
    table_used = jnp.zeros((slots,), jnp.bool_).at[place].set(True, mode="drop")
    table_val = (
        jnp.zeros((slots,), jnp.float32)
        .at[place]
        .set(codes_val.reshape(-1).astype(jnp.float32), mode="drop")
    )
    picked_rows = jnp.take(dec_weight, table_lat, axis=0)
    sent = jnp.where(table_used[:, None], picked_rows, jnp.zeros_like(picked_rows))
    received = joined_exchange(
        sent.reshape(n_lat, n_dp * cap, model), LATENT_DP, ("latent", DP), (0, 1), (0, 1)
    )
    recv_flat = received.reshape(slots, model)
    own_idx = lax.dynamic_slice_in_dim(codes_idx, device * share, share, 0).reshape(pairs)
    own_val = lax.dynamic_slice_in_dim(codes_val, device * share, share, 0)
    own_slab = own_idx // width
    hits = (own_slab[:, None] == jnp.arange(n_dev, dtype=jnp.int32)[None, :]).astype(jnp.int32)
    own_rank = jnp.sum(jnp.cumsum(hits, axis=0) * hits, axis=1) - 1
    slot_id = own_slab * cap + own_rank
    token_of = jnp.arange(pairs, dtype=jnp.int32) // topk
    select, unused_in, unused_slot = spread_codes(own_val, slot_id.reshape(share, topk), 0, slots)
    recon = jnp.dot(select, recv_flat, preferred_element_type=jnp.float32)
    resid = (recon + dec_bias - target.astype(jnp.float32)).astype(jnp.bfloat16)
    back_tokens = lax.dot_general(
        resid, recv_flat, (((1,), (1,)), ((), ())), preferred_element_type=jnp.float32
    )
    code_grad = pick_columns(back_tokens, slot_id.reshape(share, topk))
    token_table = jnp.full((slots,), share, jnp.int32).at[slot_id].set(token_of)
    padded = jnp.concatenate([resid, jnp.zeros((1, model), jnp.bfloat16)], axis=0)
    returned = jnp.take(padded, token_table, axis=0)
    back_rows = joined_exchange(
        returned.reshape(n_lat, n_dp * cap, model), LATENT_DP, ("latent", DP), (0, 1), (0, 1)
    )
    columns = jnp.arange(width, dtype=jnp.int32)[None, :]
    scaled = jnp.where(
        table_used[:, None] & (table_lat[:, None] == columns), table_val[:, None], 0.0
    ).astype(jnp.bfloat16)
    grad = lax.dot_general(
        scaled,
        back_rows.reshape(slots, model),
        (((0,), (0,)), ((), ())),
        preferred_element_type=jnp.float32,
    )
    proj = jnp.dot(
        grad, whole_basis, precision=lax.Precision.HIGHEST, preferred_element_type=jnp.float32
    )
    first_out, second_out, normed = adam_rows(proj, first_mom, second_mom)
    update = lax.dot_general(
        normed,
        whole_basis,
        (((1,), (1,)), ((), ())),
        precision=lax.Precision.HIGHEST,
        preferred_element_type=jnp.float32,
    ).astype(jnp.bfloat16)
    return (update, first_out, second_out, code_grad)


def solution(mesh):
    torus = Mesh(mesh.devices.reshape(mesh.shape["latent"], 2, 2), ("latent", "dp_0", "dp_1"))
    in_specs = (
        P(),
        P(),
        P(LATENT_DP, None),
        P(LATENT_DP, None),
        P(),
        P(DP, None),
        P(LATENT_DP, None),
        P(LATENT_DP, None),
    )
    out_specs = (P(LATENT_DP, None), P(LATENT_DP, None), P(LATENT_DP, None), P(LATENT_DP, None))
    return jax.shard_map(
        shards, mesh=torus, in_specs=in_specs, out_specs=out_specs, check_vma=False
    )
```

profile of v0, /device:TPU:1, one launch (start us, length us, event | category | flops | bytes accessed | tf_op | source)
XLA Modules:
  0.0 467.6 jit_solution(13306578422658080554)
XLA Ops:
  9.5 60.3 %scatter_custom_fusion.1 = s32[256]{0:T(256)S(1)} fusion(s32[16384]{0:T(1024)S(1)} %bitcast.80, s32[16384]{0:T(1024)S(1)} %reshape.466, s32[]{:T(128)} %constant.82.clone.1), kind=kCustom, calls=%fused_computation.74 | custom fusion | bytes 1028 | tf_op jit(solution)/shard_map/scatter | solution.py:124
  69.9 68.7 %scatter_custom_fusion = pred[256]{0:T(512)(128)(4,1)S(1)} fusion(s32[16384]{0:T(1024)S(1)} %bitcast.81, pred[16384]{0:T(1024)(128)(4,1)S(1)} %broadcast.366, pred[]{:T(512)} %constant.75.clone.1), kind=kCustom, calls=%fused_computation.63 | custom fusion | bytes 257 | tf_op jit(solution)/shard_map/scatter | solution.py:125
  138.6 8.4 %gather_fusion = bf16[256,6144]{1,0:T(8,128)(2,1)S(1)} fusion(bf16[384,6144]{1,0:T(8,128)(2,1)} %param.11, s32[1024]{0:T(1024)S(1)} %pad_clamp_fusion.1), kind=kCustom, calls=%fused_computation | custom fusion | bytes 6292480 | tf_op jit(solution)/shard_map/jit(_take)/gather | solution.py:131
  149.7 5.0 %reduce.6 = bf16[256,6144]{1,0:T(8,128)(2,1)S(1)} reduce(bf16[256,1,1,6144]{3,0,2,1:T(8,128)(2,1)} %fusion, bf16[]{:T(256)} %broadcast.395), dimensions={1,2}, to_apply=%copy.40.reduce_sub_computation | reduce | bytes 6291458 | tf_op jit(solution)/shard_map/jit(_where)/select_n | solution.py:132
  154.7 3.5 reshape.506
  158.2 15.6 %all-to-all-start = ((bf16[256,2,3072]{2,1,0:T(2,128)(2,1)}), bf16[256,2,3072]{2,1,0:T(2,128)(2,1)S(1)}, u32[]{:S(2)}, u32[]{:S(2)}) async-start(bf16[256,2,3072]{2,1,0:T(2,128)(2,1)} %reshape.506), calls=%async_computation | async-start | bytes 6291456 | tf_op jit(solution)/shard_map/all_to_all | solution.py:51
  176.6 73.9 %all-gather.5.cloned.1.call-done = f32[3072,256]{1,0:T(8,128)} async-done(((f32[1536,256]{1,0:T(8,128)}), f32[3072,256]{1,0:T(8,128)}) %all-gather.5.cloned.1.call-update) | async-done | bytes 3145744 | tf_op jit(solution)/shard_map/all_gather | solution.py:29
  250.5 7.4 %reshape.507 = bf16[256,1,1,6144]{3,2,1,0:T(2,128)(2,1)} reshape(bf16[256,2,3072]{2,1,0:T(2,128)(2,1)S(1)} %all-to-all-done) | data formatting | bytes 6291456
  257.9 18.3 %reduce.3 = bf16[256,6144]{1,0:T(8,128)(2,1)S(1)} reduce(bf16[256,1,1,6144]{3,2,1,0:T(2,128)(2,1)} %reshape.507, bf16[]{:T(256)} %constant.151), dimensions={1,2}, to_apply=%all_to_all.6.reduce_sub_computation | reduce | bytes 6291458 | tf_op jit(solution)/shard_map/all_to_all | solution.py:51
  278.8 4.5 reshape_reshape.10
  284.1 4.0 gather_fusion.1
  288.1 3.9 bitcast_select_fusion
  292.0 5.6 %reduce.7 = bf16[256,6144]{1,0:T(8,128)(2,1)} reduce(bf16[256,1,1,6144]{3,0,2,1:T(8,128)(2,1)} %bitcast_select_fusion, bf16[]{:T(256)} %broadcast.395), dimensions={1,2}, to_apply=%copy.41.reduce_sub_computation | reduce | bytes 6291458 | tf_op jit(solution)/shard_map/jit(_take)/select_n | solution.py:153
  297.6 8.0 %reshape.508 = bf16[256,2,3072]{2,1,0:T(2,128)(2,1)} reshape(bf16[256,6144]{1,0:T(8,128)(2,1)} %reduce.7) | data formatting | bytes 6291456
  305.6 12.3 %all-to-all-start.1 = ((bf16[256,2,3072]{2,1,0:T(2,128)(2,1)}), bf16[256,2,3072]{2,1,0:T(2,128)(2,1)}, u32[]{:S(2)}, u32[]{:S(2)}) async-start(bf16[256,2,3072]{2,1,0:T(2,128)(2,1)} %reshape.508), calls=%async_computation.1 | async-start | bytes 6291456 | tf_op jit(solution)/shard_map/all_to_all | solution.py:51
  318.1 60.7 %scatter_custom_fusion.2 = f32[256]{0:T(256)S(1)} fusion(s32[16384]{0:T(1024)S(1)} %bitcast.82, f32[16384]{0:T(1024)S(1)} %reshape.474, f32[]{:T(128)} %constant.132.clone.1), kind=kCustom, calls=%fused_computation.72 | custom fusion | bytes 1028 | tf_op jit(solution)/shard_map/scatter | solution.py:129
  380.5 5.8 %copy.42 = f32[2,2,1536,256]{3,2,1,0:T(8,128)} copy(f32[2,2,1536,256]{3,2,0,1:T(8,128)} %bitcast.76) | data formatting | bytes 12582912 | tf_op jit(solution)/shard_map/transpose | solution.py:32
  386.3 6.5 %all-to-all-done.1 = bf16[256,2,3072]{2,1,0:T(2,128)(2,1)} async-done(((bf16[256,2,3072]{2,1,0:T(2,128)(2,1)}), bf16[256,2,3072]{2,1,0:T(2,128)(2,1)}, u32[]{:S(2)}, u32[]{:S(2)}) %all-to-all-start.1) | async-done | bytes 3145760 | tf_op jit(solution)/shard_map/all_to_all | solution.py:51
  392.8 19.4 %reshape.509 = bf16[256,1,1,6144]{3,2,1,0:T(2,128)(2,1)} reshape(bf16[256,2,3072]{2,1,0:T(2,128)(2,1)} %all-to-all-done.1) | data formatting | bytes 6291456
  412.2 18.3 %reduce.4 = bf16[256,6144]{1,0:T(8,128)(2,1)S(1)} reduce(bf16[256,1,1,6144]{3,2,1,0:T(2,128)(2,1)} %reshape.509, bf16[]{:T(256)} %constant.151), dimensions={1,2}, to_apply=%all_to_all.7.reduce_sub_computation | reduce | bytes 6291458 | tf_op jit(solution)/shard_map/all_to_all | solution.py:51
  433.1 5.9 %reshape_reshape.11 = bf16[256,6144]{1,0:T(8,128)(2,1)} reshape(bf16[64,4,1,6144]{3,1,0,2:T(4,128)(2,1)} %bitcast.75) | data formatting | bytes 6291456 | tf_op jit(solution)/shard_map/reshape;reshape | solution.py:163
  439.0 3.6 fusion.8
  442.7 7.8 %multiply_add_fusion = (f32[384,256]{1,0:T(8,128)S(1)}, f32[384,256]{1,0:T(8,128)S(1)}) fusion(f32[384,256]{1,0:T(8,128)S(1)} %copy-done.2, f32[384,256]{1,0:T(8,128)S(1)} %copy-done.3, f32[384,6144]{1,0:T(8,128)S(1)} %fusion.8, f32[6144,256]{1,0:T(8,128)S(1)} %bitcast.72), kind=kOutput, calls=%fused_computation.17 | convolution fusion | flops 7248445440 | bytes 17301504 | tf_op jit(solution)/shard_map/dot_general | solution.py:167
  450.5 10.1 %convolution_convert_fusion = bf16[384,6144]{1,0:T(8,128)(2,1)} fusion(f32[6144,256]{1,0:T(8,128)S(1)} %bitcast.73, f32[384,256]{1,0:T(8,128)S(1)} %get-tuple-element.34, f32[384,256]{1,0:T(8,128)S(1)} %get-tuple-element.33), kind=kOutput, calls=%fused_computation.6 | convolution fusion | flops 7250509824 | bytes 11796480 | tf_op jit(solution)/shard_map/dot_general | solution.py:171
  (68 shorter events, 15.5 us)
Async XLA Ops:
  158.2 16.4 %copy-start.4 = (s32[256,64]{0,1:T(8,128)S(1)}, s32[256,64]{0,1:T(8,128)}, u32[]{:S(2)}) copy-start(s32[256,64]{0,1:T(8,128)} %param.9) | copy-start | bytes 196612
  158.2 16.8 %copy-start.5 = (bf16[256,64]{0,1:T(8,128)(2,1)S(1)}, bf16[256,64]{0,1:T(8,128)(2,1)}, u32[]{:S(2)}) copy-start(bf16[256,64]{0,1:T(8,128)(2,1)} %param.8) | copy-start | bytes 98308
  158.2 92.3 %all-to-all-start = ((bf16[256,2,3072]{2,1,0:T(2,128)(2,1)}), bf16[256,2,3072]{2,1,0:T(2,128)(2,1)S(1)}, u32[]{:S(2)}, u32[]{:S(2)}) async-start(bf16[256,2,3072]{2,1,0:T(2,128)(2,1)} %reshape.506), calls=%async_computation | async-start | bytes 6291456 | tf_op jit(solution)/shard_map/all_to_all | solution.py:51
  173.8 76.6 %all-gather.5.cloned.1.call-start = ((), (), s32[]{:S(2)}) async-start(), calls=%async_computation.2 | async-start | bytes 4718592 | tf_op jit(solution)/shard_map/all_gather | solution.py:29
  174.6 205.9 %all-gather.7.cloned.1.call-start = ((), (), s32[]{:S(2)}) async-start(), calls=%async_computation.3 | async-start | bytes 9437184 | tf_op jit(solution)/shard_map/all_gather | solution.py:29
  283.2 0.7 copy-start.6
  283.3 0.7 copy-start.7
  305.6 87.2 %all-to-all-start.1 = ((bf16[256,2,3072]{2,1,0:T(2,128)(2,1)}), bf16[256,2,3072]{2,1,0:T(2,128)(2,1)}, u32[]{:S(2)}, u32[]{:S(2)}) async-start(bf16[256,2,3072]{2,1,0:T(2,128)(2,1)} %reshape.508), calls=%async_computation.1 | async-start | bytes 6291456 | tf_op jit(solution)/shard_map/all_to_all | solution.py:51
  433.1 9.5 %slice-start = ((s8[6291456]{0:T(1024)(128)(4,1)}), s8[2097152]{0:T(1024)(128)(4,1)S(1)}, s32[]{:S(2)}) async-start(s8[6291456]{0:T(1024)(128)(4,1)} %bitcast.70), calls=%async_computation.4 | async-start | bytes 4194304
  439.0 3.6 slice-start.1
  439.0 3.6 copy-start.2
  439.0 3.6 copy-start.3
  450.4 10.1 %copy-start = (f32[384,256]{1,0:T(8,128)}, f32[384,256]{1,0:T(8,128)S(1)}, u32[]{:S(2)}) copy-start(f32[384,256]{1,0:T(8,128)S(1)} %get-tuple-element.33) | copy-start | bytes 1179652
  450.4 10.1 %copy-start.1 = (f32[384,256]{1,0:T(8,128)}, f32[384,256]{1,0:T(8,128)S(1)}, u32[]{:S(2)}) copy-start(f32[384,256]{1,0:T(8,128)S(1)} %get-tuple-element.34) | copy-start | bytes 1179652
Sparse Core Ops, SparseCore 0:
  176.5 73.9 all-gather.4
  252.2 22.3 all-gather.6
where the time goes:
time: 474 us; the launch traced here: 468 us
  local copies, waits for them, and re-layouts  264 us (56%)
  waiting for transfers between devices  81.1 us (17%)
  other arithmetic  56.6 us (12%)
  starting transfers between devices  28 us (6%)
  matrix products  22.9 us (5%)
  between operations  14.6 us (3%)
    all_gather x2, waiting for transfers between devices, gather_in_order(): pieces = lax.all_gather(pieces, axes[k])  73.9 us
    scatter x1, local copies, waits for them, and re-layouts, shards(): table_used = jnp.zeros((slots,), jnp.bool_).at[place].set(True, mode='drop')  68.7 us
    scatter x1, local copies, waits for them, and re-layouts, shards(): table_val = jnp.zeros((slots,), jnp.float32).at[place].set(codes_val.resh...  60.7 us
    scatter x1, local copies, waits for them, and re-layouts, shards(): table_lat = jnp.zeros((slots,), jnp.int32).at[place].set(local, mode='drop')  60.3 us
    unnamed x25, local copies, waits for them, and re-layouts  38.6 us
    all_to_all x2, other arithmetic, joined_exchange(): lax.all_to_all(pieces, axis, split_axis=0, concat_axis=0, tiled=True)  36.5 us
    all_to_all x2, starting transfers between devices, joined_exchange(): lax.all_to_all(pieces, axis, split_axis=0, concat_axis=0, tiled=True)  27.9 us
    dot_general x1, matrix products, shards(): lax.dot_general(normed, whole_basis, (((1,), (1,)), ((), ())), precision=...  10.1 us
  transfers between devices with their start and end apart: 4, of which 2 were waited for; matrix products, arithmetic and copies ran while one was open for 27% of the time, Pallas kernels for 0%

commit v1 on v0

v1 whole, which is shorter than its diff:
```python
import math

import jax
import jax.numpy as jnp
from jax import lax
from jax.experimental import pallas as pl
from jax.experimental.pallas import tpu as pltpu
from jax.sharding import Mesh
from jax.sharding import PartitionSpec as P

AXES = ("y", "x_hi", "z", "x_lo", "core")
PLANE = ("y", "x_hi", "x_lo", "core")
RING = ("x_hi", "x_lo", "core")

beta_one = 0.9
beta_two = 0.999
epsilon = 1e-08
first_fix = 1.0 - math.exp(100.0 * math.log(0.9))
second_fix = 1.0 - math.exp(100.0 * math.log(0.999))

LAT = 384
TOK = 256
TOPK = 64
MODEL = 6144
RANK = 256
PIECE = MODEL // 4
BF = jnp.bfloat16
F32 = jnp.float32
VMEM = pltpu.VMEM


def iota(shape, dim):
    return lax.broadcasted_iota(jnp.int32, shape, dim)


def dot_nt(a, b):
    return lax.dot_general(a, b, (((1,), (1,)), ((), ())), preferred_element_type=F32)


def slab_of(idx):
    return jnp.floor((idx.astype(F32) + 0.5) * (1.0 / LAT))


def pack_kernel(place, idx_ref, val_ref, weight_ref, sent_ref, codes_ref, hot_ref):
    @pl.when(pl.program_id(0) == 0)
    def _():
        me = place[0]
        idx = idx_ref[...]
        inside = slab_of(idx) == me.astype(F32)
        local = jnp.sum(jnp.where(inside, idx - me * LAT + 1, 0), axis=0, keepdims=True) - 1
        value = jnp.sum(
            jnp.where(inside, val_ref[...].astype(F32), 0.0), axis=0, keepdims=True
        )
        hit = iota((LAT, TOK), 0) == local
        row = iota((TOK, TOK), 0)
        token = (row >> 5) * 32 + (row & 7) * 4 + ((row >> 3) & 3)
        order = jnp.where(iota((TOK, TOK), 1) == token, 1.0, 0.0).astype(BF)
        hot_ref[...] = dot_nt(order, jnp.where(hit, 1.0, 0.0).astype(BF)).astype(BF)
        codes_ref[...] = dot_nt(jnp.where(hit, value, 0.0).astype(BF), order).astype(BF)

    sent_ref[...] = jnp.dot(
        hot_ref[...], weight_ref[...], preferred_element_type=F32
    ).astype(BF)


def pack(place, idx_t, val_t, weight):
    step = 768
    return pl.pallas_call(
        pack_kernel,
        grid_spec=pltpu.PrefetchScalarGridSpec(
            num_scalar_prefetch=1,
            grid=(MODEL // step,),
            in_specs=[
                pl.BlockSpec((TOPK, TOK), lambda j, s: (0, 0)),
                pl.BlockSpec((TOPK, TOK), lambda j, s: (0, 0)),
                pl.BlockSpec((LAT, step), lambda j, s: (0, j)),
            ],
            out_specs=[
                pl.BlockSpec((TOK, step), lambda j, s: (0, j)),
                pl.BlockSpec((LAT, TOK), lambda j, s: (0, 0)),
            ],
            scratch_shapes=[pltpu.VMEM((TOK, LAT), BF)],
        ),
        out_shape=[
            jax.ShapeDtypeStruct((TOK, MODEL), BF),
            jax.ShapeDtypeStruct((LAT, TOK), BF),
        ],
        cost_estimate=pl.CostEstimate(
            flops=2 * TOK * LAT * MODEL, bytes_accessed=8_000_000, transcendentals=0
        ),
        name="pack",
    )(place, idx_t, val_t, weight)


def recon_kernel(place, idx_ref, val_ref, recv_ref, part_ref, slab_ref):
    z = place[3]
    token = place[1] * 32 + iota((8, TOK), 0) * 4 + place[2]
    pick = jnp.where(iota((8, TOK), 1) == token, 1.0, 0.0).astype(BF)
    slab = dot_nt(pick, slab_of(idx_ref[...]).astype(BF))
    value = dot_nt(pick, val_ref[...])
    slab_ref[...] = slab
    lane = iota((8, TOK), 1)
    source = ((lane >> 5) * 32 + ((lane >> 3) & 3) + z * 4).astype(F32)
    weight = jnp.zeros((8, TOK), F32)
    for k in range(TOPK):
        weight += jnp.where(slab[:, k : k + 1] == source, value[:, k : k + 1], 0.0)
    weight = jnp.where((lane & 7) == iota((8, TOK), 0), weight, 0.0).astype(BF)
    step = 1024
    for j in range(MODEL // step):
        part_ref[:, j * step : (j + 1) * step] = jnp.dot(
            weight, recv_ref[:, j * step : (j + 1) * step], preferred_element_type=F32
        )


def whole(n):
    return [pl.BlockSpec(memory_space=pltpu.VMEM)] * n


SMEM = pl.BlockSpec(memory_space=pltpu.SMEM)


def partial_recon(place, idx_t, val_t, recv):
    return pl.pallas_call(
        recon_kernel,
        in_specs=[SMEM] + whole(3),
        out_specs=whole(2),
        out_shape=[
            jax.ShapeDtypeStruct((8, MODEL), F32),
            jax.ShapeDtypeStruct((8, TOPK), F32),
        ],
        cost_estimate=pl.CostEstimate(
            flops=2 * TOK * 8 * MODEL, bytes_accessed=4_000_000, transcendentals=0
        ),
        name="partial_recon",
    )(place, idx_t, val_t, recv)


def back_kernel(place, resid_ref, recv_ref, slab_ref, b0, b1, b2, b3, cg_ref, proj_ref):
    z = place[3]
    block = place[4]
    proj = jnp.zeros((8, RANK), F32)
    for g, ref in enumerate((b0, b1, b2, b3)):
        at = pl.multiple_of((block ^ g) * PIECE, 128)
        proj += jnp.dot(resid_ref[:, pl.ds(at, PIECE)], ref[...], preferred_element_type=F32)
    proj_ref[...] = jnp.broadcast_to(proj[None], (32, 8, RANK))
    dots = dot_nt(resid_ref[...], recv_ref[...])
    lane = iota((8, TOK), 1)
    dots = jnp.where((lane & 7) == iota((8, TOK), 0), dots, 0.0)
    member = jnp.where(iota((TOK, 128), 0) >> 3 == iota((TOK, 128), 1), 1.0, 0.0)
    dots = jnp.dot(
        dots, member, precision=lax.Precision.HIGHEST, preferred_element_type=F32
    )
    slab = slab_ref[...]
    grad = jnp.zeros((8, TOPK), F32)
    for p in range(32):
        source = ((p >> 2) * 32 + (p & 3) + z * 4).astype(F32)
        grad += jnp.where(slab == source, dots[:, p : p + 1], 0.0)
    cg_ref[:, 0:TOPK] = grad
    cg_ref[:, TOPK:] = jnp.zeros((8, 128 - TOPK), F32)


def back(place, resid, recv, slab, pieces):
    return pl.pallas_call(
        back_kernel,
        in_specs=[SMEM] + whole(7),
        out_specs=whole(2),
        out_shape=[
            jax.ShapeDtypeStruct((8, 128), F32),
            jax.ShapeDtypeStruct((32, 8, RANK), F32),
        ],
        cost_estimate=pl.CostEstimate(
            flops=2 * TOK * 8 * MODEL * 2, bytes_accessed=7_000_000, transcendentals=0
        ),
        name="back",
    )(place, resid, recv, slab, *pieces)


def update_kernel(
    place, codes_ref, proj_ref, first_ref, second_ref, b0, b1, b2, b3,
    out_ref, first_out_ref, second_out_ref, high_ref, low_ref,
):
    g = pl.program_id(0)
    j = pl.program_id(1)

    @pl.when((g == 0) & (j == 0))
    def _():
        proj_tok = proj_ref[...]
        codes = codes_ref[...]
        one = proj_tok.astype(BF)
        rest = proj_tok - one.astype(F32)
        two = rest.astype(BF)
        three = (rest - two.astype(F32)).astype(BF)
        proj = (
            jnp.dot(codes, three, preferred_element_type=F32)
            + jnp.dot(codes, two, preferred_element_type=F32)
            + jnp.dot(codes, one, preferred_element_type=F32)
        )
        first = beta_one * first_ref[...] + (1.0 - beta_one) * proj
        second = beta_two * second_ref[...] + (1.0 - beta_two) * proj * proj
        first_out_ref[...] = first
        second_out_ref[...] = second
        normed = first / first_fix / (jnp.sqrt(second / second_fix) + epsilon)
        high = normed.astype(BF)
        high_ref[...] = high
        low_ref[...] = (normed - high.astype(F32)).astype(BF)

    for n, ref in enumerate((b0, b1, b2, b3)):

        @pl.when(g == n)
        def _(ref=ref):
            rows = ref[pl.ds(pl.multiple_of(j * 768, 256), 768), :]
            out_ref[...] = (dot_nt(low_ref[...], rows) + dot_nt(high_ref[...], rows)).astype(BF)


def update(place, codes, proj, first, second, pieces):
    full = lambda shape: pl.BlockSpec(shape, lambda g, j, s: (0, 0))
    return pl.pallas_call(
        update_kernel,
        grid_spec=pltpu.PrefetchScalarGridSpec(
            num_scalar_prefetch=1,
            grid=(4, 2),
            in_specs=[full((LAT, TOK)), full((TOK, RANK)), full((LAT, RANK)), full((LAT, RANK))]
            + [full((PIECE, RANK))] * 4,
            out_specs=[
                pl.BlockSpec((LAT, 768), lambda g, j, s: (0, (s[4] ^ g) * 2 + j)),
                full((LAT, RANK)),
                full((LAT, RANK)),
            ],
            scratch_shapes=[pltpu.VMEM((LAT, RANK), BF), pltpu.VMEM((LAT, RANK), BF)],
        ),
        out_shape=[
            jax.ShapeDtypeStruct((LAT, MODEL), BF),
            jax.ShapeDtypeStruct((LAT, RANK), F32),
            jax.ShapeDtypeStruct((LAT, RANK), F32),
        ],
        cost_estimate=pl.CostEstimate(
            flops=2 * LAT * RANK * MODEL * 2, bytes_accessed=11_000_000, transcendentals=0
        ),
        name="update",
    )(place, codes, proj, first, second, *pieces)


def shards(codes_val, codes_idx, target, dec_weight, dec_bias, basis, first_mom, second_mom):
    y_x = lax.axis_index(("y", "x_hi"))
    z = lax.axis_index("z")
    block = lax.axis_index(("x_lo", "core"))
    device = (y_x * 8 + z) * 4 + block
    place = jnp.stack([device, y_x, block, z, block]).astype(jnp.int32)
    idx_t = codes_idx.T
    val_t = codes_val.T

    own = basis.astype(BF)
    pairs = []
    for x in range(4):
        pairs.append((((x + 3) % 4) * 2, x * 2))
        pairs.append((((x + 1) % 4) * 2 + 1, x * 2 + 1))
    swap = [(0, 1), (1, 0)]
    other = lax.ppermute(own, RING, pairs)
    own_sib = lax.ppermute(own, "core", swap)
    other_sib = lax.ppermute(other, "core", swap)
    pieces = (own, own_sib, other, other_sib)

    sent, codes = pack(place, idx_t, val_t, dec_weight)
    recv = lax.all_to_all(
        sent.reshape(32, 8, MODEL), PLANE, split_axis=0, concat_axis=0, tiled=True
    ).reshape(TOK, MODEL)
    part, slab = partial_recon(place, idx_t, val_t, recv)
    rows = MODEL // 128
    part = lax.all_to_all(
        part.reshape(8, rows, 128), "z", split_axis=0, concat_axis=0, tiled=True
    )
    recon = jnp.sum(part, axis=0)
    resid = (
        recon + dec_bias.reshape(rows, 128) - target.reshape(rows, 128).astype(F32)
    ).astype(BF)
    resid = lax.all_to_all(
        jnp.broadcast_to(resid[None], (8, rows, 128)), "z", split_axis=0, concat_axis=0, tiled=True
    ).reshape(8, MODEL)
    grad, proj = back(place, resid, recv, slab, pieces)
    proj = lax.all_to_all(proj, PLANE, split_axis=0, concat_axis=0, tiled=True)
    grad = lax.all_to_all(
        grad.reshape(8, 1, 128), "z", split_axis=0, concat_axis=0, tiled=True
    )
    code_grad = jnp.sum(grad, axis=0)[:, :TOPK]
    new, first_out, second_out = update(
        place, codes, proj.reshape(TOK, RANK), first_mom, second_mom, pieces
    )
    return (new, first_out, second_out, code_grad)


def solution(mesh):
    torus = Mesh(mesh.devices.reshape(4, 2, 8, 2, 2), AXES)
    rows = P(AXES, None)
    in_specs = (P(), P(), rows, rows, P(), P(("x_lo", "core"), None), rows, rows)
    return jax.shard_map(
        shards, mesh=torus, in_specs=in_specs, out_specs=(rows, rows, rows, rows), check_vma=False
    )
```

time: 474 us -> 146 us (0.31); the launches traced: 468 us -> 145 us
  local copies, waits for them, and re-layouts: 264 us -> 5.37 us
  other arithmetic: 56.6 us -> 2.97 us
  Pallas kernels: 0 us -> 27 us
  matrix products: 22.9 us -> 0 us
  waiting for transfers between devices: 81.1 us -> 59.5 us
  blocking collectives: 0 us -> 19.6 us
  between operations: 14.6 us -> 0.72 us
    scatter x4 -> x0, local copies, waits for them, and re-layouts: 191 us -> none  [the longest x1 68.7 us: shards(): table_used = jnp.zeros((slots,), jnp.bool_).at[place].set(True, mode='drop')]
    all_gather x2 -> x0, waiting for transfers between devices: 73.9 us -> none  [gather_in_order(): pieces = lax.all_gather(pieces, axes[k])]
    ppermute x0 -> x3, waiting for transfers between devices: none -> 40.4 us  [the longest x1 40.4 us: shards(): other = lax.ppermute(own, RING, pairs)]
    all_to_all x2 -> x0, other arithmetic: 36.5 us -> none  [joined_exchange(): lax.all_to_all(pieces, axis, split_axis=0, concat_axis=0, tiled=True)]
    unnamed x25 -> x9, local copies, waits for them, and re-layouts: 38.6 us -> 3.05 us
    pallas_call x0 -> x4, Pallas kernels: none -> 27 us  [the longest x1 9.64 us: update(): pl.pallas_call(update_kernel, grid_spec=pltpu.PrefetchScalarGridSpec(num_...]
    dot_general x5 -> x0, matrix products: 22.9 us -> none  [the longest x1 10.1 us: shards(): lax.dot_general(normed, whole_basis, (((1,), (1,)), ((), ())), precision=...]
    all_to_all x0 -> x2, blocking collectives: none -> 19.6 us  [the longest x1 9.82 us: shards(): lax.all_to_all(jnp.broadcast_to(resid[None], (8, rows, 128)), 'z', split_...]
  transfers between devices with their start and end apart: 4 -> 6, of which waited for: 2 -> 3; matrix products, arithmetic and copies ran while one was open for 27% -> 4% of each run, Pallas kernels for 0% -> 2%
where the time goes in v1:
time: 146 us; the launch traced here: 145 us
  waiting for transfers between devices  59.5 us (41%)
  starting transfers between devices  30.3 us (21%)
  Pallas kernels  27 us (18%)
  blocking collectives  19.6 us (13%)
  local copies, waits for them, and re-layouts  5.37 us (4%)
  other arithmetic  2.97 us (2%)
    ppermute x1, waiting for transfers between devices, shards(): other = lax.ppermute(own, RING, pairs)  40.4 us
    all_to_all x1, waiting for transfers between devices, shards(): lax.all_to_all(part.reshape(8, rows, 128), 'z', split_axis=0, concat_axis...  10.8 us
    all_to_all x1, blocking collectives, shards(): lax.all_to_all(jnp.broadcast_to(resid[None], (8, rows, 128)), 'z', split_...  9.82 us
    all_to_all x1, blocking collectives, shards(): lax.all_to_all(grad.reshape(8, 1, 128), 'z', split_axis=0, concat_axis=0,...  9.74 us
    all_to_all x1, starting transfers between devices, shards(): proj = lax.all_to_all(proj, PLANE, split_axis=0, concat_axis=0, tiled=True)  9.73 us
    pallas_call x1, Pallas kernels, update(): pl.pallas_call(update_kernel, grid_spec=pltpu.PrefetchScalarGridSpec(num_...  9.64 us
    pallas_call x1, Pallas kernels, pack(): pl.pallas_call(pack_kernel, grid_spec=pltpu.PrefetchScalarGridSpec(num_sc...  8.68 us
    all_to_all x1, starting transfers between devices, shards(): lax.all_to_all(sent.reshape(32, 8, MODEL), PLANE, split_axis=0, concat_ax...  8.58 us
  transfers between devices with their start and end apart: 6, of which 3 were waited for; matrix products, arithmetic and copies ran while one was open for 4% of the time, Pallas kernels for 2%

profile of v1, /device:TPU:1, one launch (start us, length us, event | category | flops | bytes accessed | tf_op | source)
XLA Modules:
  0.0 145.4 jit_solution(9073767355440510492)
XLA Ops:
  0.6 0.7 stack.20.place
  1.3 8.7 %pack.1 = (bf16[256,6144]{1,0:T(8,128)(2,1)}, bf16[384,256]{1,0:T(8,128)(2,1)}) custom-call(s32[5]{0:T(128)} %stack.20.place, s32[64,256]{1,0:T(8,128)} %bitcast.31, bf16[64,256]{1,0:T(8,128)(2,1)} %bitcast.35, bf16[384,6144]{1,0:T(8,128)(2,1)} %weight_ref.1), custom_call_target="tpu_custom_call" | custom-call | flops 1207959552 | bytes 8000000 | tf_op jit(solution)/shard_map/pack/pallas_call | solution.py:68
  10.0 8.6 %all-to-all-start = ((bf16[32,8,6144]{2,1,0:T(8,128)(2,1)}), bf16[32,8,6144]{2,1,0:T(8,128)(2,1)S(1)}, u32[]{:S(2)}, u32[]{:S(2)}) async-start(bf16[32,8,6144]{2,1,0:T(8,128)(2,1)} %bitcast.28), calls=%async_computation | async-start | bytes 6291456 | tf_op jit(solution)/shard_map/all_to_all | solution.py:264
  18.6 0.0 copy-start.2
  18.6 0.0 copy-start.3
  18.6 2.4 %convert_element_type.23.b0 = bf16[1536,256]{1,0:T(8,128)(2,1)} convert(f32[1536,256]{1,0:T(8,128)} %param.13) | non-fusion elementwise | flops 393216 | bytes 2359296 | tf_op jit(solution)/shard_map/convert_element_type | solution.py:252
  21.0 2.6 %collective-permute-start.1 = (bf16[1536,256]{1,0:T(8,128)(2,1)}, bf16[1536,256]{1,0:T(8,128)(2,1)}, u32[]{:S(2)}, u32[]{:S(2)}) collective-permute-start(bf16[1536,256]{1,0:T(8,128)(2,1)} %convert_element_type.23.b0), channel_id=1, source_target_pairs={{34,0},{3,1},{0,2},{33,3},{2,32},{35,33},{32,34},{1,35},{38,4},{7,... | collective-permute-start | bytes 2359304 | tf_op jit(solution)/shard_map/ppermute | solution.py:258
  23.5 0.0 collective-permute-start
  23.5 40.4 %collective-permute-done.1.b2 = bf16[1536,256]{1,0:T(8,128)(2,1)} collective-permute-done((bf16[1536,256]{1,0:T(8,128)(2,1)}, bf16[1536,256]{1,0:T(8,128)(2,1)}, u32[]{:S(2)}, u32[]{:S(2)}) %collective-permute-start.1) | collective-permute-done | bytes 786464 | tf_op jit(solution)/shard_map/ppermute | solution.py:258
  63.9 1.2 collective-permute-start.2
  65.1 1.7 %copy-done = bf16[32,8,6144]{2,1,0:T(8,128)(2,1)} copy-done((bf16[32,8,6144]{2,1,0:T(8,128)(2,1)}, bf16[32,8,6144]{2,1,0:T(8,128)(2,1)S(1)}, u32[]{:S(2)}) %copy-start) | copy-done | bytes 3145752
  66.8 3.5 %partial_recon.1 = (f32[8,6144]{1,0:T(8,128)}, f32[8,64]{1,0:T(8,128)}) custom-call(s32[5]{0:T(128)} %stack.20.place, s32[64,256]{1,0:T(8,128)} %bitcast.32, bf16[64,256]{1,0:T(8,128)(2,1)} %bitcast.36, bf16[256,6144]{1,0:T(8,128)(2,1)} %bitcast.26), custom_call_target="tpu_custom_call" | custom-call | flops 25165824 | bytes 4000000 | tf_op jit(solution)/shard_map/partial_recon/pallas_call | solution.py:123
  70.3 1.6 %copy.12 = f32[8,48,128]{2,1,0:T(8,128)} copy(f32[8,48,128]{2,0,1:T(8,128)} %bitcast.34) | data formatting | bytes 393216 | tf_op jit(solution)/shard_map/reshape | solution.py:270
  72.0 8.2 %all-to-all-start.1 = ((f32[8,48,128]{2,1,0:T(8,128)}), f32[8,48,128]{2,1,0:T(8,128)S(1)}, u32[]{:S(2)}, u32[]{:S(2)}) async-start(f32[8,48,128]{2,1,0:T(8,128)} %copy.12), calls=%async_computation.1 | async-start | bytes 393216 | tf_op jit(solution)/shard_map/all_to_all | solution.py:269
  80.2 10.8 %all-to-all-done.1 = f32[8,48,128]{2,1,0:T(8,128)S(1)} async-done(((f32[8,48,128]{2,1,0:T(8,128)}), f32[8,48,128]{2,1,0:T(8,128)S(1)}, u32[]{:S(2)}, u32[]{:S(2)}) %all-to-all-start.1) | async-done | bytes 196640 | tf_op jit(solution)/shard_map/all_to_all | solution.py:269
  91.0 9.8 %all_to_all.25 = bf16[8,48,128]{2,1,0:T(8,128)(2,1)S(1)} all-to-all(bf16[8,48,128]{2,1,0:T(8,128)(2,1)S(1)} %broadcast_in_dim.2), channel_id=1, replica_groups=mesh['y'=4,'x_hi'=2,'z'=8,'x_lo'=2,'core'=2] {'z'}, dimensions={0} | all-to-all | bytes 196608 | tf_op jit(solution)/shard_map/all_to_all | solution.py:276
  100.8 0.7 copy.16
  101.5 5.2 %back.1 = (f32[8,128]{1,0:T(8,128)}, f32[32,8,256]{2,1,0:T(8,128)}) custom-call(s32[5]{0:T(128)} %stack.20.place, bf16[8,6144]{1,0:T(8,128)(2,1)} %bitcast.30, bf16[256,6144]{1,0:T(8,128)(2,1)} %bitcast.27, f32[8,64]{1,0:T(8,128)} %get-tuple-element.16.slab_ref, bf16[1536,256]{1,0:T(8,128)(2,1)} %convert_element_type.23.b0, ...), custom_call_target="tpu_custom_call" | custom-call | flops 50331648 | bytes 7000000 | tf_op jit(solution)/shard_map/back/pallas_call | solution.py:163
  106.7 9.7 %all_to_all.26 = f32[8,1,128]{2,1,0:T(1,128)S(1)} all-to-all(f32[8,1,128]{2,1,0:T(1,128)} %bitcast.38), channel_id=1, replica_groups=mesh['y'=4,'x_hi'=2,'z'=8,'x_lo'=2,'core'=2] {'z'}, dimensions={0} | all-to-all | bytes 8192 | tf_op jit(solution)/shard_map/all_to_all | solution.py:281
  116.4 9.7 %all-to-all-start.3 = ((f32[32,8,256]{2,1,0:T(8,128)}), f32[32,8,256]{2,1,0:T(8,128)S(1)}, u32[]{:S(2)}, u32[]{:S(2)}) async-start(f32[32,8,256]{2,1,0:T(8,128)} %get-tuple-element.17), calls=%async_computation.3 | async-start | bytes 524288 | tf_op jit(solution)/shard_map/all_to_all | solution.py:280
  126.1 0.5 reduce_sum.21
  126.7 8.3 %all-to-all-done.3 = f32[32,8,256]{2,1,0:T(8,128)S(1)} async-done(((f32[32,8,256]{2,1,0:T(8,128)}), f32[32,8,256]{2,1,0:T(8,128)S(1)}, u32[]{:S(2)}, u32[]{:S(2)}) %all-to-all-start.3) | async-done | bytes 262176 | tf_op jit(solution)/shard_map/all_to_all | solution.py:280
  135.0 0.7 copy-done.1
  135.7 9.6 %update.1 = (bf16[384,6144]{1,0:T(8,128)(2,1)}, f32[384,256]{1,0:T(8,128)}, f32[384,256]{1,0:T(8,128)}) custom-call(s32[5]{0:T(128)} %stack.20.place, bf16[384,256]{1,0:T(8,128)(2,1)} %get-tuple-element.13.codes_ref, f32[256,256]{1,0:T(8,128)} %bitcast.33, f32[384,256]{1,0:T(8,128)} %first_ref.1, f32[384,256]{1,0:T(8,128)} %second_ref.1, ...), custom_call_target="tpu_custom_call" | custom-call | flops 2415919104 | bytes 11000000 | tf_op jit(solution)/shard_map/update/pallas_call | solution.py:217
  (11 shorter events, 0.1 us)
Async XLA Ops:
  10.0 55.1 %all-to-all-start = ((bf16[32,8,6144]{2,1,0:T(8,128)(2,1)}), bf16[32,8,6144]{2,1,0:T(8,128)(2,1)S(1)}, u32[]{:S(2)}, u32[]{:S(2)}) async-start(bf16[32,8,6144]{2,1,0:T(8,128)(2,1)} %bitcast.28), calls=%async_computation | async-start | bytes 6291456 | tf_op jit(solution)/shard_map/all_to_all | solution.py:264
  18.6 61.6 %copy-start.2 = (bf16[1,6144]{1,0:T(2,128)(2,1)S(1)}, bf16[1,6144]{1,0:T(2,128)(2,1)}, u32[]{:S(2)}) copy-start(bf16[1,6144]{1,0:T(2,128)(2,1)} %param.10) | copy-start | bytes 36868
  18.6 72.4 %copy-start.3 = (f32[6144]{0:T(1024)S(1)}, f32[6144]{0:T(1024)}, u32[]{:S(2)}) copy-start(f32[6144]{0:T(1024)} %param.12) | copy-start | bytes 73732
  21.0 42.9 %collective-permute-start.1 = (bf16[1536,256]{1,0:T(8,128)(2,1)}, bf16[1536,256]{1,0:T(8,128)(2,1)}, u32[]{:S(2)}, u32[]{:S(2)}) collective-permute-start(bf16[1536,256]{1,0:T(8,128)(2,1)} %convert_element_type.23.b0), channel_id=1, source_target_pairs={{34,0},{3,1},{0,2},{33,3},{2,32},{35,33},{32,34},{1,35},{38,4},{7,... | collective-permute-start | bytes 2359304 | tf_op jit(solution)/shard_map/ppermute | solution.py:258
  23.5 78.0 %collective-permute-start = (bf16[1536,256]{1,0:T(8,128)(2,1)}, bf16[1536,256]{1,0:T(8,128)(2,1)}, u32[]{:S(2)}, u32[]{:S(2)}) collective-permute-start(bf16[1536,256]{1,0:T(8,128)(2,1)} %convert_element_type.23.b0), channel_id=1, source_target_pairs={{0,1},{1,0},{2,3},{3,2},{4,5},{5,4},{6,7},{7,6},{8,9},{9,8},{10,11... | collective-permute-start | bytes 2359304 | tf_op jit(solution)/shard_map/ppermute | solution.py:259
  63.9 37.6 %collective-permute-start.2 = (bf16[1536,256]{1,0:T(8,128)(2,1)}, bf16[1536,256]{1,0:T(8,128)(2,1)}, u32[]{:S(2)}, u32[]{:S(2)}) collective-permute-start(bf16[1536,256]{1,0:T(8,128)(2,1)} %collective-permute-done.1.b2), channel_id=1, source_target_pairs={{0,1},{1,0},{2,3},{3,2},{4,5},{5,4},{6,7},{7,6},{8,9},{9,8},{10,11... | collective-permute-start | bytes 2359304 | tf_op jit(solution)/shard_map/ppermute | solution.py:260
  65.1 1.7 %copy-start = (bf16[32,8,6144]{2,1,0:T(8,128)(2,1)}, bf16[32,8,6144]{2,1,0:T(8,128)(2,1)S(1)}, u32[]{:S(2)}) copy-start(bf16[32,8,6144]{2,1,0:T(8,128)(2,1)S(1)} %all-to-all-done) | copy-start | bytes 9437188
  72.0 19.0 %all-to-all-start.1 = ((f32[8,48,128]{2,1,0:T(8,128)}), f32[8,48,128]{2,1,0:T(8,128)S(1)}, u32[]{:S(2)}, u32[]{:S(2)}) async-start(f32[8,48,128]{2,1,0:T(8,128)} %copy.12), calls=%async_computation.1 | async-start | bytes 393216 | tf_op jit(solution)/shard_map/all_to_all | solution.py:269
  116.4 18.6 %all-to-all-start.3 = ((f32[32,8,256]{2,1,0:T(8,128)}), f32[32,8,256]{2,1,0:T(8,128)S(1)}, u32[]{:S(2)}, u32[]{:S(2)}) async-start(f32[32,8,256]{2,1,0:T(8,128)} %get-tuple-element.17), calls=%async_computation.3 | async-start | bytes 524288 | tf_op jit(solution)/shard_map/all_to_all | solution.py:280
  135.0 0.7 copy-start.1

commit v2 on v1

--- a/solution.py
+++ b/solution.py
@@ -7,6 +7,7 @@
 from jax.experimental.pallas import tpu as pltpu
 from jax.sharding import Mesh
 from jax.sharding import PartitionSpec as P
+
 
 AXES = ("y", "x_hi", "z", "x_lo", "core")
 PLANE = ("y", "x_hi", "x_lo", "core")
@@ -26,7 +27,6 @@
 PIECE = MODEL // 4
 BF = jnp.bfloat16
 F32 = jnp.float32
-VMEM = pltpu.VMEM
 
 
 def iota(shape, dim):
@@ -41,10 +41,18 @@
     return jnp.floor((idx.astype(F32) + 0.5) * (1.0 / LAT))
 
 
-def pack_kernel(place, idx_ref, val_ref, weight_ref, sent_ref, codes_ref, hot_ref):
+def where_am_i():
+    y_x = lax.axis_index("y") * 2 + lax.axis_index("x_hi")
+    z = lax.axis_index("z")
+    block = lax.axis_index("x_lo") * 2 + lax.axis_index("core")
+    return y_x, z, block
+
+
+def pack_kernel(idx_ref, val_ref, weight_ref, sent_ref, codes_ref, hot_ref):
     @pl.when(pl.program_id(0) == 0)
     def _():
-        me = place[0]
+        y_x, z, block = where_am_i()
+        me = (y_x * 8 + z) * 4 + block
         idx = idx_ref[...]
         inside = slab_of(idx) == me.astype(F32)
         local = jnp.sum(jnp.where(inside, idx - me * LAT + 1, 0), axis=0, keepdims=True) - 1
@@ -63,24 +71,21 @@
     ).astype(BF)
 
 
-def pack(place, idx_t, val_t, weight):
+def pack(idx_t, val_t, weight):
     step = 768
     return pl.pallas_call(
         pack_kernel,
-        grid_spec=pltpu.PrefetchScalarGridSpec(
-            num_scalar_prefetch=1,
-            grid=(MODEL // step,),
-            in_specs=[
-                pl.BlockSpec((TOPK, TOK), lambda j, s: (0, 0)),
-                pl.BlockSpec((TOPK, TOK), lambda j, s: (0, 0)),
-                pl.BlockSpec((LAT, step), lambda j, s: (0, j)),
-            ],
-            out_specs=[
-                pl.BlockSpec((TOK, step), lambda j, s: (0, j)),
-                pl.BlockSpec((LAT, TOK), lambda j, s: (0, 0)),
-            ],
-            scratch_shapes=[pltpu.VMEM((TOK, LAT), BF)],
-        ),
+        grid=(MODEL // step,),
+        in_specs=[
+            pl.BlockSpec((TOPK, TOK), lambda j: (0, 0)),
+            pl.BlockSpec((TOPK, TOK), lambda j: (0, 0)),
+            pl.BlockSpec((LAT, step), lambda j: (0, j)),
+        ],
+        out_specs=[
+            pl.BlockSpec((TOK, step), lambda j: (0, j)),
+            pl.BlockSpec((LAT, TOK), lambda j: (0, 0)),
+        ],
+        scratch_shapes=[pltpu.VMEM((TOK, LAT), BF)],
         out_shape=[
             jax.ShapeDtypeStruct((TOK, MODEL), BF),
             jax.ShapeDtypeStruct((LAT, TOK), BF),
@@ -89,12 +94,12 @@
             flops=2 * TOK * LAT * MODEL, bytes_accessed=8_000_000, transcendentals=0
         ),
         name="pack",
-    )(place, idx_t, val_t, weight)
-
-
-def recon_kernel(place, idx_ref, val_ref, recv_ref, part_ref, slab_ref):
-    z = place[3]
-    token = place[1] * 32 + iota((8, TOK), 0) * 4 + place[2]
+    )(idx_t, val_t, weight)
+
+
+def recon_kernel(idx_ref, val_ref, recv_ref, part_ref, slab_ref):
+    y_x, z, block = where_am_i()
+    token = y_x * 32 + iota((8, TOK), 0) * 4 + block
     pick = jnp.where(iota((8, TOK), 1) == token, 1.0, 0.0).astype(BF)
     slab = dot_nt(pick, slab_of(idx_ref[...]).astype(BF))
     value = dot_nt(pick, val_ref[...])
@@ -107,42 +112,58 @@
     weight = jnp.where((lane & 7) == iota((8, TOK), 0), weight, 0.0).astype(BF)
     step = 1024
     for j in range(MODEL // step):
-        part_ref[:, j * step : (j + 1) * step] = jnp.dot(
+        part = jnp.dot(
             weight, recv_ref[:, j * step : (j + 1) * step], preferred_element_type=F32
         )
+        for c in range(step // 128):
+            part_ref[:, j * (step // 128) + c, :] = part[:, c * 128 : (c + 1) * 128]
 
 
 def whole(n):
     return [pl.BlockSpec(memory_space=pltpu.VMEM)] * n
 
 
-SMEM = pl.BlockSpec(memory_space=pltpu.SMEM)
-
-
-def partial_recon(place, idx_t, val_t, recv):
+def partial_recon(idx_t, val_t, recv):
     return pl.pallas_call(
         recon_kernel,
-        in_specs=[SMEM] + whole(3),
+        in_specs=whole(3),
         out_specs=whole(2),
         out_shape=[
-            jax.ShapeDtypeStruct((8, MODEL), F32),
+            jax.ShapeDtypeStruct((8, MODEL // 128, 128), F32),
             jax.ShapeDtypeStruct((8, TOPK), F32),
         ],
         cost_estimate=pl.CostEstimate(
             flops=2 * TOK * 8 * MODEL, bytes_accessed=4_000_000, transcendentals=0
         ),
+        compiler_params=pltpu.CompilerParams(vmem_limit_bytes=10 * 1024 * 1024),
         name="partial_recon",
-    )(place, idx_t, val_t, recv)
-
-
-def back_kernel(place, resid_ref, recv_ref, slab_ref, b0, b1, b2, b3, cg_ref, proj_ref):
-    z = place[3]
-    block = place[4]
+    )(idx_t, val_t, recv)
+
+
+def project_kernel(resid_ref, b0, b1, b2, b3, proj_ref):
+    _, _, block = where_am_i()
     proj = jnp.zeros((8, RANK), F32)
     for g, ref in enumerate((b0, b1, b2, b3)):
         at = pl.multiple_of((block ^ g) * PIECE, 128)
         proj += jnp.dot(resid_ref[:, pl.ds(at, PIECE)], ref[...], preferred_element_type=F32)
     proj_ref[...] = jnp.broadcast_to(proj[None], (32, 8, RANK))
+
+
+def project(resid, pieces):
+    return pl.pallas_call(
+        project_kernel,
+        in_specs=whole(5),
+        out_specs=whole(1)[0],
+        out_shape=jax.ShapeDtypeStruct((32, 8, RANK), F32),
+        cost_estimate=pl.CostEstimate(
+            flops=2 * RANK * 8 * MODEL, bytes_accessed=3_500_000, transcendentals=0
+        ),
+        name="project",
+    )(resid, *pieces)
+
+
+def back_kernel(resid_ref, recv_ref, slab_ref, cg_ref):
+    _, z, _ = where_am_i()
     dots = dot_nt(resid_ref[...], recv_ref[...])
     lane = iota((8, TOK), 1)
     dots = jnp.where((lane & 7) == iota((8, TOK), 0), dots, 0.0)
@@ -159,20 +180,18 @@
     cg_ref[:, TOPK:] = jnp.zeros((8, 128 - TOPK), F32)
 
 
-def back(place, resid, recv, slab, pieces):
+def back(resid, recv, slab):
     return pl.pallas_call(
         back_kernel,
-        in_specs=[SMEM] + whole(7),
-        out_specs=whole(2),
-        out_shape=[
-            jax.ShapeDtypeStruct((8, 128), F32),
-            jax.ShapeDtypeStruct((32, 8, RANK), F32),
-        ],
-        cost_estimate=pl.CostEstimate(
-            flops=2 * TOK * 8 * MODEL * 2, bytes_accessed=7_000_000, transcendentals=0
-        ),
+        in_specs=whole(3),
+        out_specs=whole(1)[0],
+        out_shape=jax.ShapeDtypeStruct((8, 128), F32),
+        cost_estimate=pl.CostEstimate(
+            flops=2 * TOK * 8 * MODEL, bytes_accessed=3_500_000, transcendentals=0
+        ),
+        compiler_params=pltpu.CompilerParams(vmem_limit_bytes=10 * 1024 * 1024),
         name="back",
-    )(place, resid, recv, slab, *pieces)
+    )(resid, recv, slab)
 
 
 def update_kernel(
@@ -222,7 +241,7 @@
             in_specs=[full((LAT, TOK)), full((TOK, RANK)), full((LAT, RANK)), full((LAT, RANK))]
             + [full((PIECE, RANK))] * 4,
             out_specs=[
-                pl.BlockSpec((LAT, 768), lambda g, j, s: (0, (s[4] ^ g) * 2 + j)),
+                pl.BlockSpec((LAT, 768), lambda g, j, s: (0, (s[0] ^ g) * 2 + j)),
                 full((LAT, RANK)),
                 full((LAT, RANK)),
             ],
@@ -240,47 +259,36 @@
     )(place, codes, proj, first, second, *pieces)
 
 
-def shards(codes_val, codes_idx, target, dec_weight, dec_bias, basis, first_mom, second_mom):
-    y_x = lax.axis_index(("y", "x_hi"))
-    z = lax.axis_index("z")
-    block = lax.axis_index(("x_lo", "core"))
-    device = (y_x * 8 + z) * 4 + block
-    place = jnp.stack([device, y_x, block, z, block]).astype(jnp.int32)
+def step(codes_val, codes_idx, target, dec_weight, dec_bias, basis, first_mom, second_mom):
+    block = lax.axis_index(("x_lo", "core")).astype(jnp.int32)
+    place = block[None]
     idx_t = codes_idx.T
     val_t = codes_val.T
-
-    own = basis.astype(BF)
+    exchange = lambda a, axes: lax.all_to_all(a, axes, split_axis=0, concat_axis=0, tiled=True)
+    swap = [(0, 1), (1, 0)]
     pairs = []
     for x in range(4):
         pairs.append((((x + 3) % 4) * 2, x * 2))
         pairs.append((((x + 1) % 4) * 2 + 1, x * 2 + 1))
-    swap = [(0, 1), (1, 0)]
-    other = lax.ppermute(own, RING, pairs)
+
+    sent, codes = pack(idx_t, val_t, dec_weight)
+    recv = exchange(sent.reshape(32, 8, MODEL), PLANE).reshape(TOK, MODEL)
+    own = basis.astype(BF)
     own_sib = lax.ppermute(own, "core", swap)
+    part, slab = partial_recon(idx_t, val_t, recv)
+    late, recv = lax.optimization_barrier((own, recv))
+    other = lax.ppermute(late, RING, pairs)
     other_sib = lax.ppermute(other, "core", swap)
     pieces = (own, own_sib, other, other_sib)
-
-    sent, codes = pack(place, idx_t, val_t, dec_weight)
-    recv = lax.all_to_all(
-        sent.reshape(32, 8, MODEL), PLANE, split_axis=0, concat_axis=0, tiled=True
-    ).reshape(TOK, MODEL)
-    part, slab = partial_recon(place, idx_t, val_t, recv)
     rows = MODEL // 128
-    part = lax.all_to_all(
-        part.reshape(8, rows, 128), "z", split_axis=0, concat_axis=0, tiled=True
-    )
+    part = exchange(part, "z")
     recon = jnp.sum(part, axis=0)
-    resid = (
-        recon + dec_bias.reshape(rows, 128) - target.reshape(rows, 128).astype(F32)
-    ).astype(BF)
-    resid = lax.all_to_all(
-        jnp.broadcast_to(resid[None], (8, rows, 128)), "z", split_axis=0, concat_axis=0, tiled=True
-    ).reshape(8, MODEL)
-    grad, proj = back(place, resid, recv, slab, pieces)
-    proj = lax.all_to_all(proj, PLANE, split_axis=0, concat_axis=0, tiled=True)
-    grad = lax.all_to_all(
-        grad.reshape(8, 1, 128), "z", split_axis=0, concat_axis=0, tiled=True
-    )
+    resid = (recon + dec_bias.reshape(rows, 128) - target.reshape(rows, 128).astype(F32)).astype(BF)
+    resid = exchange(jnp.broadcast_to(resid[None], (8, rows, 128)), "z").reshape(8, MODEL)
+    proj = project(resid, pieces)
+    proj = exchange(proj, PLANE)
+    grad = back(resid, recv, slab)
+    grad = exchange(grad.reshape(8, 1, 128), "z")
     code_grad = jnp.sum(grad, axis=0)[:, :TOPK]
     new, first_out, second_out = update(
         place, codes, proj.reshape(TOK, RANK), first_mom, second_mom, pieces
@@ -293,5 +301,5 @@
     rows = P(AXES, None)
     in_specs = (P(), P(), rows, rows, P(), P(("x_lo", "core"), None), rows, rows)
     return jax.shard_map(
-        shards, mesh=torus, in_specs=in_specs, out_specs=(rows, rows, rows, rows), check_vma=False
+        step, mesh=torus, in_specs=in_specs, out_specs=(rows, rows, rows, rows), check_vma=False
     )

time: 146 us -> 141 us (0.966)
  blocking collectives: 19.6 us -> 9.82 us
  waiting for transfers between devices: 59.5 us -> 68.8 us
  local copies, waits for them, and re-layouts: 5.37 us -> 0.76 us
  starting transfers between devices: 30.3 us -> 33.8 us
  Pallas kernels: 27 us -> 23.6 us
    all_to_all x3 -> x4, waiting for transfers between devices: 19.1 us -> 59.8 us  [step(): lax.all_to_all(a, axes, split_axis=0, concat_axis=0, tiled=True)]
    ppermute x3, waiting for transfers between devices: 40.4 us -> 9.01 us  [the longest x1 9 us: step(): other = lax.ppermute(late, RING, pairs)]
    all_to_all x2 -> x1, blocking collectives: 19.6 us -> 9.82 us  [step(): lax.all_to_all(a, axes, split_axis=0, concat_axis=0, tiled=True)]
    ppermute x3, starting transfers between devices: 3.76 us -> 6.96 us  [the longest x1 4.51 us: step(): other_sib = lax.ppermute(other, 'core', swap)]
    pallas_call x3 -> x4, Pallas kernels: 17.4 us -> 14.7 us  [the longest x1 8.03 us: pack(): pl.pallas_call(pack_kernel, grid=(MODEL // step,), in_specs=[pl.BlockSpec...]
    unnamed x9 -> x13, local copies, waits for them, and re-layouts: 3.05 us -> 0.75 us
    reshape x1 -> x0, local copies, waits for them, and re-layouts: 1.64 us -> none  [shards(): part.reshape(8, rows, 128)]
    all_to_all x3 -> x4, starting transfers between devices: 26.5 us -> 26.9 us  [step(): lax.all_to_all(a, axes, split_axis=0, concat_axis=0, tiled=True)]
  transfers between devices with their start and end apart: 6 -> 7, of which waited for: 3 -> 5; matrix products, arithmetic and copies ran while one was open for 4% -> 2% of each run, Pallas kernels for 2% -> 5%
where the time goes in v2:
time: 141 us
  waiting for transfers between devices  68.8 us (49%)
  starting transfers between devices  33.8 us (24%)
  Pallas kernels  23.6 us (17%)
  blocking collectives  9.82 us (7%)
  other arithmetic  2.99 us (2%)
    all_to_all x4, waiting for transfers between devices, step(): lax.all_to_all(a, axes, split_axis=0, concat_axis=0, tiled=True)  59.8 us
    all_to_all x4, starting transfers between devices, step(): lax.all_to_all(a, axes, split_axis=0, concat_axis=0, tiled=True)  26.9 us
    all_to_all x1, blocking collectives, step(): lax.all_to_all(a, axes, split_axis=0, concat_axis=0, tiled=True)  9.82 us
    ppermute x1, waiting for transfers between devices, step(): other = lax.ppermute(late, RING, pairs)  9 us
    pallas_call x1, Pallas kernels, update(): pl.pallas_call(update_kernel, grid_spec=pltpu.PrefetchScalarGridSpec(num_...  8.92 us
    pallas_call x1, Pallas kernels, pack(): pl.pallas_call(pack_kernel, grid=(MODEL // step,), in_specs=[pl.BlockSpec...  8.03 us
    ppermute x1, starting transfers between devices, step(): other_sib = lax.ppermute(other, 'core', swap)  4.51 us
    pallas_call x1, Pallas kernels, project(): pl.pallas_call(project_kernel, in_specs=whole(5), out_specs=whole(1)[0],...  3.12 us
  transfers between devices with their start and end apart: 7, of which 5 were waited for; matrix products, arithmetic and copies ran while one was open for 2% of the time, Pallas kernels for 5%

profile of v2, /device:TPU:1, one launch (start us, length us, event | category | flops | bytes accessed | tf_op | source)
XLA Modules:
  0.0 140.6 jit_solution(8042095955620375974)
XLA Ops:
  0.6 8.0 %pack.1 = (bf16[256,6144]{1,0:T(8,128)(2,1)}, bf16[384,256]{1,0:T(8,128)(2,1)}) custom-call(s32[64,256]{1,0:T(8,128)} %bitcast.26, bf16[64,256]{1,0:T(8,128)(2,1)} %bitcast.28, bf16[384,6144]{1,0:T(8,128)(2,1)} %weight_ref.1), custom_call_target="tpu_custom_call" | custom-call | flops 1207959552 | bytes 8000000 | tf_op jit(solution)/shard_map/pack/pallas_call | solution.py:76
  8.7 8.7 %all-to-all-start = ((bf16[32,8,6144]{2,1,0:T(8,128)(2,1)}), bf16[32,8,6144]{2,1,0:T(8,128)(2,1)S(1)}, u32[]{:S(2)}, u32[]{:S(2)}) async-start(bf16[32,8,6144]{2,1,0:T(8,128)(2,1)} %bitcast.30), calls=%async_computation | async-start | bytes 6291456 | tf_op jit(solution)/shard_map/all_to_all | solution.py:267
  17.4 0.0 copy-start.4
  17.4 0.0 copy-start.5
  17.4 2.4 %convert_element_type.23.b0 = bf16[1536,256]{1,0:T(8,128)(2,1)} convert(f32[1536,256]{1,0:T(8,128)} %param.13) | non-fusion elementwise | flops 393216 | bytes 2359296 | tf_op jit(solution)/shard_map/convert_element_type | solution.py:276
  19.8 37.4 %all-to-all-done = bf16[32,8,6144]{2,1,0:T(8,128)(2,1)S(1)} async-done(((bf16[32,8,6144]{2,1,0:T(8,128)(2,1)}), bf16[32,8,6144]{2,1,0:T(8,128)(2,1)S(1)}, u32[]{:S(2)}, u32[]{:S(2)}) %all-to-all-start) | async-done | bytes 3145760 | tf_op jit(solution)/shard_map/all_to_all | solution.py:267
  57.2 1.5 %collective-permute-start.1 = (bf16[1536,256]{1,0:T(8,128)(2,1)}, bf16[1536,256]{1,0:T(8,128)(2,1)}, u32[]{:S(2)}, u32[]{:S(2)}) collective-permute-start(bf16[1536,256]{1,0:T(8,128)(2,1)} %convert_element_type.23.b0), channel_id=1, source_target_pairs={{34,0},{3,1},{0,2},{33,3},{2,32},{35,33},{32,34},{1,35},{38,4},{7,... | collective-permute-start | bytes 2359304 | tf_op jit(solution)/shard_map/ppermute | solution.py:280
  58.7 1.0 collective-permute-start
  59.6 9.0 %collective-permute-done.1.b2 = bf16[1536,256]{1,0:T(8,128)(2,1)} collective-permute-done((bf16[1536,256]{1,0:T(8,128)(2,1)}, bf16[1536,256]{1,0:T(8,128)(2,1)}, u32[]{:S(2)}, u32[]{:S(2)}) %collective-permute-start.1) | collective-permute-done | bytes 786464 | tf_op jit(solution)/shard_map/ppermute | solution.py:280
  68.6 4.5 %collective-permute-start.2 = (bf16[1536,256]{1,0:T(8,128)(2,1)}, bf16[1536,256]{1,0:T(8,128)(2,1)}, u32[]{:S(2)}, u32[]{:S(2)}) collective-permute-start(bf16[1536,256]{1,0:T(8,128)(2,1)} %collective-permute-done.1.b2), channel_id=1, source_target_pairs={{0,1},{1,0},{2,3},{3,2},{4,5},{5,4},{6,7},{7,6},{8,9},{9,8},{10,11... | collective-permute-start | bytes 2359304 | tf_op jit(solution)/shard_map/ppermute | solution.py:281
  73.1 1.6 %partial_recon.1 = (f32[8,48,128]{2,1,0:T(8,128)}, f32[8,64]{1,0:T(8,128)S(1)}) custom-call(s32[64,256]{1,0:T(8,128)S(1)} %bitcast.27, bf16[64,256]{1,0:T(8,128)(2,1)S(1)} %bitcast.29, bf16[256,6144]{1,0:T(8,128)(2,1)S(1)} %bitcast.22), custom_call_target="tpu_custom_call" | custom-call | flops 25165824 | bytes 4000000 | tf_op jit(solution)/shard_map/partial_recon/pallas_call | solution.py:127
  74.7 8.2 %all-to-all-start.1 = ((f32[8,48,128]{2,1,0:T(8,128)}), f32[8,48,128]{2,1,0:T(8,128)S(1)}, u32[]{:S(2)}, u32[]{:S(2)}) async-start(f32[8,48,128]{2,1,0:T(8,128)} %get-tuple-element.15), calls=%async_computation.1 | async-start | bytes 393216 | tf_op jit(solution)/shard_map/all_to_all | solution.py:267
  83.0 10.8 %all-to-all-done.1 = f32[8,48,128]{2,1,0:T(8,128)S(1)} async-done(((f32[8,48,128]{2,1,0:T(8,128)}), f32[8,48,128]{2,1,0:T(8,128)S(1)}, u32[]{:S(2)}, u32[]{:S(2)}) %all-to-all-start.1) | async-done | bytes 196640 | tf_op jit(solution)/shard_map/all_to_all | solution.py:267
  93.8 9.8 %all_to_all.25 = bf16[8,48,128]{2,1,0:T(8,128)(2,1)S(1)} all-to-all(bf16[8,48,128]{2,1,0:T(8,128)(2,1)S(1)} %broadcast_in_dim.10), channel_id=1, replica_groups=mesh['y'=4,'x_hi'=2,'z'=8,'x_lo'=2,'core'=2] {'z'}, dimensions={0} | all-to-all | bytes 196608 | tf_op jit(solution)/shard_map/all_to_all | solution.py:267
  103.7 0.0 copy-start
  103.7 1.9 %back.1 = f32[8,128]{1,0:T(8,128)} custom-call(bf16[8,6144]{1,0:T(8,128)(2,1)S(1)} %bitcast.24, bf16[256,6144]{1,0:T(8,128)(2,1)S(1)} %bitcast.23, f32[8,64]{1,0:T(8,128)S(1)} %get-tuple-element.21.slab_ref), custom_call_target="tpu_custom_call" | custom-call | flops 25165824 | bytes 3500000 | tf_op jit(solution)/shard_map/back/pallas_call | solution.py:184
  105.6 3.3 %all-to-all-start.4 = ((f32[8,1,128]{2,1,0:T(1,128)}), f32[8,1,128]{2,1,0:T(1,128)S(1)}, u32[]{:S(2)}, u32[]{:S(2)}) async-start(f32[8,1,128]{2,1,0:T(1,128)} %bitcast.9), calls=%async_computation.4 | async-start | bytes 8192 | tf_op jit(solution)/shard_map/all_to_all | solution.py:267
  108.9 3.1 %project.1 = f32[32,8,256]{2,1,0:T(8,128)} custom-call(bf16[8,6144]{1,0:T(8,128)(2,1)} %bitcast.25, bf16[1536,256]{1,0:T(8,128)(2,1)} %convert_element_type.23.b0, bf16[1536,256]{1,0:T(8,128)(2,1)} %collective-permute-done.b1, bf16[1536,256]{1,0:T(8,128)(2,1)} %collective-permute-done.1.b2, bf16[1536,256]{1,0:T(8,128)(2,1)} %collective-permute-done.2.b3), custom_call_target="tpu_custom_call" | custom-call | flops 25165824 | bytes 3500000 | tf_op jit(solution)/shard_map/project/pallas_call | solution.py:153
  112.0 3.3 %all-to-all-done.4 = f32[8,1,128]{2,1,0:T(1,128)S(1)} async-done(((f32[8,1,128]{2,1,0:T(1,128)}), f32[8,1,128]{2,1,0:T(1,128)S(1)}, u32[]{:S(2)}, u32[]{:S(2)}) %all-to-all-start.4) | async-done | bytes 4128 | tf_op jit(solution)/shard_map/all_to_all | solution.py:267
  115.3 6.7 %all-to-all-start.3 = ((f32[32,8,256]{2,1,0:T(8,128)}), f32[32,8,256]{2,1,0:T(8,128)S(1)}, u32[]{:S(2)}, u32[]{:S(2)}) async-start(f32[32,8,256]{2,1,0:T(8,128)} %project.1), calls=%async_computation.3 | async-start | bytes 524288 | tf_op jit(solution)/shard_map/all_to_all | solution.py:267
  122.0 0.5 reduce_sum.21
  122.5 8.4 %all-to-all-done.3 = f32[32,8,256]{2,1,0:T(8,128)S(1)} async-done(((f32[32,8,256]{2,1,0:T(8,128)}), f32[32,8,256]{2,1,0:T(8,128)S(1)}, u32[]{:S(2)}, u32[]{:S(2)}) %all-to-all-start.3) | async-done | bytes 262176 | tf_op jit(solution)/shard_map/all_to_all | solution.py:267
  131.0 0.7 copy-done.3
  131.7 8.9 %update.1 = (bf16[384,6144]{1,0:T(8,128)(2,1)}, f32[384,256]{1,0:T(8,128)}, f32[384,256]{1,0:T(8,128)}) custom-call(s32[1]{0:T(128)} %bitcast.place, bf16[384,256]{1,0:T(8,128)(2,1)} %get-tuple-element.13.codes_ref, f32[256,256]{1,0:T(8,128)} %bitcast.32, f32[384,256]{1,0:T(8,128)} %first_ref.1, f32[384,256]{1,0:T(8,128)} %second_ref.1, ...), custom_call_target="tpu_custom_call" | custom-call | flops 2415919104 | bytes 11000000 | tf_op jit(solution)/shard_map/update/pallas_call | solution.py:236
  (15 shorter events, 0.1 us)
Async XLA Ops:
  8.7 64.5 %copy-start.1 = (s32[256,64]{0,1:T(8,128)S(1)}, s32[256,64]{0,1:T(8,128)}, u32[]{:S(2)}) copy-start(s32[256,64]{0,1:T(8,128)} %param.9) | copy-start | bytes 196612
  8.7 64.5 %copy-start.2 = (bf16[256,64]{0,1:T(8,128)(2,1)S(1)}, bf16[256,64]{0,1:T(8,128)(2,1)}, u32[]{:S(2)}) copy-start(bf16[256,64]{0,1:T(8,128)(2,1)} %param.8) | copy-start | bytes 98308
  8.7 48.5 %all-to-all-start = ((bf16[32,8,6144]{2,1,0:T(8,128)(2,1)}), bf16[32,8,6144]{2,1,0:T(8,128)(2,1)S(1)}, u32[]{:S(2)}, u32[]{:S(2)}) async-start(bf16[32,8,6144]{2,1,0:T(8,128)(2,1)} %bitcast.30), calls=%async_computation | async-start | bytes 6291456 | tf_op jit(solution)/shard_map/all_to_all | solution.py:267
  17.4 65.6 %copy-start.4 = (bf16[1,6144]{1,0:T(2,128)(2,1)S(1)}, bf16[1,6144]{1,0:T(2,128)(2,1)}, u32[]{:S(2)}) copy-start(bf16[1,6144]{1,0:T(2,128)(2,1)} %param.10) | copy-start | bytes 36868
  17.4 76.4 %copy-start.5 = (f32[6144]{0:T(1024)S(1)}, f32[6144]{0:T(1024)}, u32[]{:S(2)}) copy-start(f32[6144]{0:T(1024)} %param.12) | copy-start | bytes 73732
  57.2 11.5 %collective-permute-start.1 = (bf16[1536,256]{1,0:T(8,128)(2,1)}, bf16[1536,256]{1,0:T(8,128)(2,1)}, u32[]{:S(2)}, u32[]{:S(2)}) collective-permute-start(bf16[1536,256]{1,0:T(8,128)(2,1)} %convert_element_type.23.b0), channel_id=1, source_target_pairs={{34,0},{3,1},{0,2},{33,3},{2,32},{35,33},{32,34},{1,35},{38,4},{7,... | collective-permute-start | bytes 2359304 | tf_op jit(solution)/shard_map/ppermute | solution.py:280
  58.7 50.2 %collective-permute-start = (bf16[1536,256]{1,0:T(8,128)(2,1)}, bf16[1536,256]{1,0:T(8,128)(2,1)}, u32[]{:S(2)}, u32[]{:S(2)}) collective-permute-start(bf16[1536,256]{1,0:T(8,128)(2,1)} %convert_element_type.23.b0), channel_id=1, source_target_pairs={{0,1},{1,0},{2,3},{3,2},{4,5},{5,4},{6,7},{7,6},{8,9},{9,8},{10,11... | collective-permute-start | bytes 2359304 | tf_op jit(solution)/shard_map/ppermute | solution.py:277
  68.6 40.3 %collective-permute-start.2 = (bf16[1536,256]{1,0:T(8,128)(2,1)}, bf16[1536,256]{1,0:T(8,128)(2,1)}, u32[]{:S(2)}, u32[]{:S(2)}) collective-permute-start(bf16[1536,256]{1,0:T(8,128)(2,1)} %collective-permute-done.1.b2), channel_id=1, source_target_pairs={{0,1},{1,0},{2,3},{3,2},{4,5},{5,4},{6,7},{7,6},{8,9},{9,8},{10,11... | collective-permute-start | bytes 2359304 | tf_op jit(solution)/shard_map/ppermute | solution.py:281
  74.7 19.0 %all-to-all-start.1 = ((f32[8,48,128]{2,1,0:T(8,128)}), f32[8,48,128]{2,1,0:T(8,128)S(1)}, u32[]{:S(2)}, u32[]{:S(2)}) async-start(f32[8,48,128]{2,1,0:T(8,128)} %get-tuple-element.15), calls=%async_computation.1 | async-start | bytes 393216 | tf_op jit(solution)/shard_map/all_to_all | solution.py:267
  103.7 5.3 %copy-start = (bf16[1,8,48,128]{3,1,2,0:T(8,128)(2,1)}, bf16[1,8,48,128]{3,1,2,0:T(8,128)(2,1)S(1)}, u32[]{:S(2)}) copy-start(bf16[1,8,48,128]{3,1,2,0:T(8,128)(2,1)S(1)} %copy.15) | copy-start | bytes 294916
  105.6 9.7 %all-to-all-start.4 = ((f32[8,1,128]{2,1,0:T(1,128)}), f32[8,1,128]{2,1,0:T(1,128)S(1)}, u32[]{:S(2)}, u32[]{:S(2)}) async-start(f32[8,1,128]{2,1,0:T(1,128)} %bitcast.9), calls=%async_computation.4 | async-start | bytes 8192 | tf_op jit(solution)/shard_map/all_to_all | solution.py:267
  115.3 15.7 %all-to-all-start.3 = ((f32[32,8,256]{2,1,0:T(8,128)}), f32[32,8,256]{2,1,0:T(8,128)S(1)}, u32[]{:S(2)}, u32[]{:S(2)}) async-start(f32[32,8,256]{2,1,0:T(8,128)} %project.1), calls=%async_computation.3 | async-start | bytes 524288 | tf_op jit(solution)/shard_map/all_to_all | solution.py:267
  131.0 0.7 copy-start.3

commit v3 on v2

v3 whole, which is shorter than its diff:
```python
import math

import jax
import jax.numpy as jnp
from jax import lax
from jax.experimental import pallas as pl
from jax.experimental.pallas import tpu as pltpu
from jax.sharding import Mesh
from jax.sharding import PartitionSpec as P


AXES = ("y", "x_hi", "z", "x_lo", "core")
PLANE = ("y", "x_hi", "x_lo", "core")
RING = ("x_hi", "x_lo", "core")

beta_one = 0.9
beta_two = 0.999
epsilon = 1e-08
first_fix = 1.0 - math.exp(100.0 * math.log(0.9))
second_fix = 1.0 - math.exp(100.0 * math.log(0.999))

LAT = 384
TOK = 256
TOPK = 64
MODEL = 6144
RANK = 256
PIECE = MODEL // 4
PACK = 4
BF = jnp.bfloat16
F32 = jnp.float32


def iota(shape, dim):
    return lax.broadcasted_iota(jnp.int32, shape, dim)


def dot_nt(a, b):
    return lax.dot_general(a, b, (((1,), (1,)), ((), ())), preferred_element_type=F32)


def slab_of(idx):
    return jnp.floor((idx.astype(F32) + 0.5) * (1.0 / LAT))


def whole(n):
    return [pl.BlockSpec(memory_space=pltpu.VMEM)] * n


def where_am_i():
    y_x = lax.axis_index("y") * 2 + lax.axis_index("x_hi")
    z = lax.axis_index("z")
    block = lax.axis_index("x_lo") * 2 + lax.axis_index("core")
    return y_x, z, block


def pack_kernel(
    idx_hbm, val_hbm, weight_ref, sent_ref, codes_hbm,
    idx_ref, val_ref, codes_ref, in_ref, out_ref, in_sem, out_sem, sem,
):
    width = MODEL // PACK
    cuts = [pl.ds(c * width, width) for c in range(PACK)]
    loads = [
        pltpu.make_async_copy(weight_ref.at[:, cut], in_ref.at[:, cut], in_sem.at[c])
        for c, cut in enumerate(cuts)
    ]
    stores = [
        pltpu.make_async_copy(out_ref.at[:, cut], sent_ref.at[:, cut], out_sem.at[c])
        for c, cut in enumerate(cuts)
    ]
    tables = [
        pltpu.make_async_copy(idx_hbm, idx_ref, sem.at[0]),
        pltpu.make_async_copy(val_hbm, val_ref, sem.at[1]),
    ]
    for load in tables + loads:
        load.start()
    for load in tables:
        load.wait()
    y_x, z, block = where_am_i()
    me = (y_x * 8 + z) * 4 + block
    idx = idx_ref[...]
    inside = slab_of(idx) == me.astype(F32)
    local = jnp.sum(jnp.where(inside, idx - me * LAT + 1, 0), axis=0, keepdims=True) - 1
    value = jnp.sum(jnp.where(inside, val_ref[...].astype(F32), 0.0), axis=0, keepdims=True)
    hit = iota((LAT, TOK), 0) == local
    row = iota((TOK, TOK), 0)
    token = (row >> 5) * 32 + (row & 7) * 4 + ((row >> 3) & 3)
    order = jnp.where(iota((TOK, TOK), 1) == token, 1.0, 0.0).astype(BF)
    hot = dot_nt(order, jnp.where(hit, 1.0, 0.0).astype(BF)).astype(BF)
    for c, cut in enumerate(cuts):
        loads[c].wait()
        out_ref[:, cut] = jnp.dot(
            hot, in_ref[:, cut], preferred_element_type=F32
        ).astype(BF)
        stores[c].start()
    codes_ref[...] = dot_nt(jnp.where(hit, value, 0.0).astype(BF), order).astype(BF)
    store = pltpu.make_async_copy(codes_ref, codes_hbm, sem.at[2])
    store.start()
    for store in stores + [store]:
        store.wait()


ANY = pl.BlockSpec(memory_space=pl.ANY)


def pack(idx_t, val_t, weight):
    return pl.pallas_call(
        pack_kernel,
        in_specs=[ANY] * 3,
        out_specs=[ANY] * 2,
        out_shape=[
            jax.ShapeDtypeStruct((TOK, MODEL), BF),
            jax.ShapeDtypeStruct((LAT, TOK), BF),
        ],
        scratch_shapes=[
            pltpu.VMEM((TOPK, TOK), jnp.int32),
            pltpu.VMEM((TOPK, TOK), BF),
            pltpu.VMEM((LAT, TOK), BF),
            pltpu.VMEM((LAT, MODEL), BF),
            pltpu.VMEM((TOK, MODEL), BF),
            pltpu.SemaphoreType.DMA((PACK,)),
            pltpu.SemaphoreType.DMA((PACK,)),
            pltpu.SemaphoreType.DMA((3,)),
        ],
        cost_estimate=pl.CostEstimate(
            flops=2 * TOK * LAT * MODEL, bytes_accessed=8_000_000, transcendentals=0
        ),
        name="pack",
    )(idx_t, val_t, weight)


def recon_kernel(idx_ref, val_ref, recv_ref, part_ref, slab_ref):
    y_x, z, block = where_am_i()
    token = y_x * 32 + iota((8, TOK), 0) * 4 + block
    pick = jnp.where(iota((8, TOK), 1) == token, 1.0, 0.0).astype(BF)
    slab = dot_nt(pick, slab_of(idx_ref[...]).astype(BF))
    value = dot_nt(pick, val_ref[...])
    slab_ref[...] = slab
    lane = iota((8, TOK), 1)
    source = ((lane >> 5) * 32 + ((lane >> 3) & 3) + z * 4).astype(F32)
    weight = jnp.zeros((8, TOK), F32)
    for k in range(TOPK):
        weight += jnp.where(slab[:, k : k + 1] == source, value[:, k : k + 1], 0.0)
    weight = jnp.where((lane & 7) == iota((8, TOK), 0), weight, 0.0).astype(BF)
    step = 1024
    for j in range(MODEL // step):
        part = jnp.dot(
            weight, recv_ref[:, j * step : (j + 1) * step], preferred_element_type=F32
        )
        for c in range(step // 128):
            part_ref[:, j * (step // 128) + c, :] = part[:, c * 128 : (c + 1) * 128]


def partial_recon(idx_t, val_t, recv):
    return pl.pallas_call(
        recon_kernel,
        in_specs=whole(3),
        out_specs=whole(2),
        out_shape=[
            jax.ShapeDtypeStruct((8, MODEL // 128, 128), F32),
            jax.ShapeDtypeStruct((8, TOPK), F32),
        ],
        cost_estimate=pl.CostEstimate(
            flops=2 * TOK * 8 * MODEL, bytes_accessed=4_000_000, transcendentals=0
        ),
        compiler_params=pltpu.CompilerParams(vmem_limit_bytes=10 * 1024 * 1024),
        name="partial_recon",
    )(idx_t, val_t, recv)


def resid_kernel(part_ref, bias_ref, target_ref, resid_ref):
    recon = jnp.sum(part_ref[...], axis=0)
    resid = recon + bias_ref[...] - target_ref[...].astype(F32)
    resid_ref[...] = jnp.broadcast_to(resid.astype(BF)[None], resid_ref.shape)


def residual(part, bias, target):
    return pl.pallas_call(
        resid_kernel,
        in_specs=whole(3),
        out_specs=whole(1)[0],
        out_shape=jax.ShapeDtypeStruct((8, MODEL // 128, 128), BF),
        cost_estimate=pl.CostEstimate(
            flops=10 * MODEL, bytes_accessed=400_000, transcendentals=0
        ),
        compiler_params=pltpu.CompilerParams(vmem_limit_bytes=10 * 1024 * 1024),
        name="residual",
    )(part, bias, target)


def load_pieces(sources, buf_ref, sem):
    loads = [
        pltpu.make_async_copy(source, buf_ref.at[n], sem.at[n])
        for n, source in enumerate(sources)
    ]
    for load in loads:
        load.start()
    return loads


PIECES = [pltpu.VMEM((4, PIECE, RANK), BF), pltpu.SemaphoreType.DMA((4,))]


def project_kernel(resid_ref, b0, b1, b2, b3, proj_ref):
    _, _, block = where_am_i()
    proj = jnp.zeros((8, RANK), F32)
    for n, ref in enumerate((b0, b1, b2, b3)):
        at = pl.multiple_of((block ^ n) * PIECE, 128)
        proj += jnp.dot(resid_ref[:, pl.ds(at, PIECE)], ref[...], preferred_element_type=F32)
    proj_ref[...] = jnp.broadcast_to(proj[None], (32, 8, RANK))


def project(resid, pieces):
    return pl.pallas_call(
        project_kernel,
        in_specs=whole(5),
        out_specs=whole(1)[0],
        out_shape=jax.ShapeDtypeStruct((32, 8, RANK), F32),
        cost_estimate=pl.CostEstimate(
            flops=2 * RANK * 8 * MODEL, bytes_accessed=3_500_000, transcendentals=0
        ),
        name="project",
    )(resid, *pieces)


def back_kernel(resid_ref, recv_ref, slab_ref, cg_ref):
    _, z, _ = where_am_i()
    dots = dot_nt(resid_ref[...], recv_ref[...])
    lane = iota((8, TOK), 1)
    dots = jnp.where((lane & 7) == iota((8, TOK), 0), dots, 0.0)
    member = jnp.where(iota((TOK, 128), 0) >> 3 == iota((TOK, 128), 1), 1.0, 0.0)
    dots = jnp.dot(
        dots, member, precision=lax.Precision.HIGHEST, preferred_element_type=F32
    )
    slab = slab_ref[...]
    grad = jnp.zeros((8, TOPK), F32)
    for p in range(32):
        source = ((p >> 2) * 32 + (p & 3) + z * 4).astype(F32)
        grad += jnp.where(slab == source, dots[:, p : p + 1], 0.0)
    cg_ref[:, 0:TOPK] = grad
    cg_ref[:, TOPK:] = jnp.zeros((8, 128 - TOPK), F32)


def back(resid, recv, slab):
    return pl.pallas_call(
        back_kernel,
        in_specs=whole(3),
        out_specs=whole(1)[0],
        out_shape=jax.ShapeDtypeStruct((8, 128), F32),
        cost_estimate=pl.CostEstimate(
            flops=2 * TOK * 8 * MODEL, bytes_accessed=3_500_000, transcendentals=0
        ),
        compiler_params=pltpu.CompilerParams(vmem_limit_bytes=10 * 1024 * 1024),
        name="back",
    )(resid, recv, slab)


def update_kernel(
    codes_hbm, proj_hbm, first_ref, second_ref, b0, b1, b2, b3,
    new_ref, first_out_ref, second_out_ref,
    codes_ref, proj_ref, out_ref, mom_in_ref, mom_out_ref, sem, mom_sem, buf_ref, buf_sem,
):
    _, _, block = where_am_i()
    tables = [
        pltpu.make_async_copy(proj_hbm, proj_ref, mom_sem.at[4]),
        pltpu.make_async_copy(codes_hbm, codes_ref, mom_sem.at[5]),
    ]
    moments = [
        pltpu.make_async_copy(first_ref, mom_in_ref.at[0], mom_sem.at[0]),
        pltpu.make_async_copy(second_ref, mom_in_ref.at[1], mom_sem.at[1]),
    ]
    for load in tables + moments:
        load.start()
    loads = load_pieces((b0, b1, b2, b3), buf_ref, buf_sem)
    for load in tables:
        load.wait()
    proj_tok = proj_ref[...]
    codes = codes_ref[...]
    one = proj_tok.astype(BF)
    rest = proj_tok - one.astype(F32)
    two = rest.astype(BF)
    three = (rest - two.astype(F32)).astype(BF)
    proj = (
        jnp.dot(codes, three, preferred_element_type=F32)
        + jnp.dot(codes, two, preferred_element_type=F32)
        + jnp.dot(codes, one, preferred_element_type=F32)
    )
    for load in moments:
        load.wait()
    first = beta_one * mom_in_ref[0] + (1.0 - beta_one) * proj
    second = beta_two * mom_in_ref[1] + (1.0 - beta_two) * proj * proj
    mom_out_ref[0] = first
    mom_out_ref[1] = second
    stores = [
        pltpu.make_async_copy(mom_out_ref.at[0], first_out_ref, mom_sem.at[2]),
        pltpu.make_async_copy(mom_out_ref.at[1], second_out_ref, mom_sem.at[3]),
    ]
    for store in stores:
        store.start()
    normed = first / first_fix / (jnp.sqrt(second / second_fix) + epsilon)
    high = normed.astype(BF)
    low = (normed - high.astype(F32)).astype(BF)
    width = PIECE // 2
    for n in range(4):
        loads[n].wait()
        for j in range(2):
            rows = buf_ref[n, j * width : (j + 1) * width, :]
            cut = pl.ds((2 * n + j) * width, width)
            out_ref[:, cut] = (dot_nt(low, rows) + dot_nt(high, rows)).astype(BF)
            at = pl.multiple_of((block ^ n) * PIECE + j * width, 128)
            store = pltpu.make_async_copy(
                out_ref.at[:, cut], new_ref.at[:, pl.ds(at, width)], sem.at[2 * n + j]
            )
            store.start()
            stores.append(store)
    for store in stores:
        store.wait()


def update(codes, proj, first, second, pieces):
    return pl.pallas_call(
        update_kernel,
        in_specs=[ANY] * 8,
        out_specs=[ANY] * 3,
        out_shape=[
            jax.ShapeDtypeStruct((LAT, MODEL), BF),
            jax.ShapeDtypeStruct((LAT, RANK), F32),
            jax.ShapeDtypeStruct((LAT, RANK), F32),
        ],
        scratch_shapes=[
            pltpu.VMEM((LAT, TOK), BF),
            pltpu.VMEM((TOK, RANK), F32),
            pltpu.VMEM((LAT, MODEL), BF),
            pltpu.VMEM((2, LAT, RANK), F32),
            pltpu.VMEM((2, LAT, RANK), F32),
            pltpu.SemaphoreType.DMA((8,)),
            pltpu.SemaphoreType.DMA((6,)),
        ]
        + PIECES,
        cost_estimate=pl.CostEstimate(
            flops=2 * LAT * RANK * MODEL * 2, bytes_accessed=11_000_000, transcendentals=0
        ),
        name="update",
    )(codes, proj, first, second, *pieces)


def step(codes_val, codes_idx, target, dec_weight, dec_bias, basis, first_mom, second_mom):
    idx_t = codes_idx.T
    val_t = codes_val.T
    exchange = lambda a, axes: lax.all_to_all(a, axes, split_axis=0, concat_axis=0, tiled=True)
    swap = [(0, 1), (1, 0)]
    straight = []
    crossed = []
    for x in range(4):
        left = ((x + 3) % 4) * 2
        right = ((x + 1) % 4) * 2 + 1
        straight += [(left, x * 2), (right, x * 2 + 1)]
        crossed += [(right - 1, x * 2 + 1), (left + 1, x * 2)]

    rows = MODEL // 128
    sent, codes = pack(idx_t, val_t, dec_weight)
    recv = exchange(sent.reshape(32, 8, MODEL), PLANE).reshape(TOK, MODEL)
    own = basis.astype(BF)
    own_sib = lax.ppermute(own, "core", swap)
    part, slab = partial_recon(idx_t, val_t, recv)
    target = target.reshape(rows, 128)
    late, recv, target = lax.optimization_barrier((own, recv, target))
    other = lax.ppermute(late, RING, straight)
    other_sib = lax.ppermute(late, RING, crossed)
    pieces = (own, own_sib, other, other_sib)
    part = exchange(part, "z")
    resid = residual(part, dec_bias.reshape(rows, 128), target)
    resid = exchange(resid, "z").reshape(8, MODEL)
    proj = project(resid, pieces)
    proj = exchange(proj, PLANE)
    grad = back(resid, recv, slab)
    grad = exchange(grad.reshape(8, 1, 128), "z")
    code_grad = jnp.sum(grad, axis=0)[:, :TOPK]
    new, first_out, second_out = update(
        codes, proj.reshape(TOK, RANK), first_mom, second_mom, pieces
    )
    return (new, first_out, second_out, code_grad)


def solution(mesh):
    torus = Mesh(mesh.devices.reshape(4, 2, 8, 2, 2), AXES)
    rows = P(AXES, None)
    in_specs = (P(), P(), rows, rows, P(), P(("x_lo", "core"), None), rows, rows)
    return jax.shard_map(
        step, mesh=torus, in_specs=in_specs, out_specs=(rows, rows, rows, rows), check_vma=False
    )
```

time: 141 us -> 123 us (0.87)
  waiting for transfers between devices: 68.8 us -> 48.7 us
  blocking collectives: 9.82 us -> 27.1 us
  starting transfers between devices: 33.8 us -> 24 us
  Pallas kernels: 23.6 us -> 18.4 us
    all_to_all x1 -> x2, blocking collectives: 9.82 us -> 27.1 us  [step(): lax.all_to_all(a, axes, split_axis=0, concat_axis=0, tiled=True)]
    all_to_all x4 -> x3, waiting for transfers between devices: 59.8 us -> 48.7 us  [step(): lax.all_to_all(a, axes, split_axis=0, concat_axis=0, tiled=True)]
    ppermute x2, waiting for transfers between devices: 9.01 us -> 0.01 us  [the longest x1 0.01 us: step(): other = lax.ppermute(late, RING, straight)]
    all_to_all x4 -> x3, starting transfers between devices: 26.9 us -> 18.8 us  [step(): lax.all_to_all(a, axes, split_axis=0, concat_axis=0, tiled=True)]
    pallas_call x2 -> x3, Pallas kernels: 17 us -> 12.4 us  [the longest x1 6.85 us: update(): pl.pallas_call(update_kernel, in_specs=[ANY] * 8, out_specs=[ANY] * 3, ou...]
  transfers between devices with their start and end apart: 7 -> 6, of which waited for: 5 -> 3; matrix products, arithmetic and copies ran while one was open for 2% -> 2% of each run, Pallas kernels for 5% -> 5%
where the time goes in v3:
time: 123 us
  waiting for transfers between devices  48.7 us (40%)
  blocking collectives  27.1 us (22%)
  starting transfers between devices  24 us (20%)
  Pallas kernels  18.4 us (15%)
  other arithmetic  2.98 us (2%)
    all_to_all x3, waiting for transfers between devices, step(): lax.all_to_all(a, axes, split_axis=0, concat_axis=0, tiled=True)  48.7 us
    all_to_all x2, blocking collectives, step(): lax.all_to_all(a, axes, split_axis=0, concat_axis=0, tiled=True)  27.1 us
    all_to_all x3, starting transfers between devices, step(): lax.all_to_all(a, axes, split_axis=0, concat_axis=0, tiled=True)  18.8 us
    pallas_call x1, Pallas kernels, update(): pl.pallas_call(update_kernel, in_specs=[ANY] * 8, out_specs=[ANY] * 3, ou...  6.85 us
    pallas_call x1, Pallas kernels, pack(): pl.pallas_call(pack_kernel, in_specs=[ANY] * 3, out_specs=[ANY] * 2, out_...  5.56 us
    ppermute x1, starting transfers between devices, step(): other = lax.ppermute(late, RING, straight)  3.33 us
    pallas_call x1, Pallas kernels, project(): pl.pallas_call(project_kernel, in_specs=whole(5), out_specs=whole(1)[0],...  3.12 us
  transfers between devices with their start and end apart: 6, of which 3 were waited for; matrix products, arithmetic and copies ran while one was open for 2% of the time, Pallas kernels for 5%

profile of v3, /device:TPU:1, one launch (start us, length us, event | category | flops | bytes accessed | tf_op | source)
XLA Modules:
  0.0 122.6 jit_solution(7199758738906656111)
XLA Ops:
  0.6 5.6 %pack.1 = (bf16[256,6144]{1,0:T(8,128)(2,1)}, bf16[384,256]{1,0:T(8,128)(2,1)}) custom-call(s32[64,256]{1,0:T(8,128)} %bitcast.20, bf16[64,256]{1,0:T(8,128)(2,1)} %bitcast.22, bf16[384,6144]{1,0:T(8,128)(2,1)} %weight_ref.1), custom_call_target="tpu_custom_call" | custom-call | flops 1207959552 | bytes 8000000 | tf_op jit(solution)/shard_map/pack/pallas_call | solution.py:106
  6.2 0.0 copy-start.5
  6.2 0.0 copy-start.1
  6.2 0.0 copy-start.2
  6.2 8.7 %all-to-all-start = ((bf16[32,8,6144]{2,1,0:T(8,128)(2,1)}), bf16[32,8,6144]{2,1,0:T(8,128)(2,1)S(1)}, u32[]{:S(2)}, u32[]{:S(2)}) async-start(bf16[32,8,6144]{2,1,0:T(8,128)(2,1)} %bitcast.26), calls=%async_computation | async-start | bytes 6291456 | tf_op jit(solution)/shard_map/all_to_all | solution.py:349
  15.0 0.0 copy-start.3
  15.0 2.4 %convert_element_type.3.b0 = bf16[1536,256]{1,0:T(8,128)(2,1)} convert(f32[1536,256]{1,0:T(8,128)} %param.13) | non-fusion elementwise | flops 393216 | bytes 2359296 | tf_op jit(solution)/shard_map/convert_element_type | solution.py:362
  17.4 0.2 collective-permute-start
  17.6 0.1 reduce.1
  17.7 37.1 %all-to-all-done = bf16[32,8,6144]{2,1,0:T(8,128)(2,1)S(1)} async-done(((bf16[32,8,6144]{2,1,0:T(8,128)(2,1)}), bf16[32,8,6144]{2,1,0:T(8,128)(2,1)S(1)}, u32[]{:S(2)}, u32[]{:S(2)}) %all-to-all-start) | async-done | bytes 3145760 | tf_op jit(solution)/shard_map/all_to_all | solution.py:349
  54.8 1.7 %collective-permute-start.2 = (bf16[1536,256]{1,0:T(8,128)(2,1)}, bf16[1536,256]{1,0:T(8,128)(2,1)}, u32[]{:S(2)}, u32[]{:S(2)}) collective-permute-start(bf16[1536,256]{1,0:T(8,128)(2,1)} %convert_element_type.3.b0), channel_id=1, source_target_pairs={{2,1},{35,0},{32,3},{1,2},{34,33},{3,32},{0,35},{33,34},{6,5},{39,... | collective-permute-start | bytes 2359304 | tf_op jit(solution)/shard_map/ppermute | solution.py:368
  56.4 3.3 %collective-permute-start.1 = (bf16[1536,256]{1,0:T(8,128)(2,1)}, bf16[1536,256]{1,0:T(8,128)(2,1)}, u32[]{:S(2)}, u32[]{:S(2)}) collective-permute-start(bf16[1536,256]{1,0:T(8,128)(2,1)} %convert_element_type.3.b0), channel_id=1, source_target_pairs={{34,0},{3,1},{0,2},{33,3},{2,32},{35,33},{32,34},{1,35},{38,4},{7,... | collective-permute-start | bytes 2359304 | tf_op jit(solution)/shard_map/ppermute | solution.py:367
  59.8 0.9 partial_recon.1
  60.7 16.9 %all_to_all.25.part_ref = f32[8,48,128]{2,1,0:T(8,128)S(1)} all-to-all(f32[8,48,128]{2,1,0:T(8,128)S(1)} %get-tuple-element.16), channel_id=1, replica_groups=mesh['y'=4,'x_hi'=2,'z'=8,'x_lo'=2,'core'=2] {'z'}, dimensions={0} | all-to-all | bytes 393216 | tf_op jit(solution)/shard_map/all_to_all | solution.py:349
  77.6 10.2 %all_to_all.26 = bf16[8,48,128]{2,1,0:T(8,128)(2,1)S(1)} all-to-all(bf16[8,48,128]{2,1,0:T(8,128)(2,1)S(1)} %residual.1), channel_id=1, replica_groups=mesh['y'=4,'x_hi'=2,'z'=8,'x_lo'=2,'core'=2] {'z'}, dimensions={0} | all-to-all | bytes 196608 | tf_op jit(solution)/shard_map/all_to_all | solution.py:349
  87.9 1.9 %back.1 = f32[8,128]{1,0:T(8,128)} custom-call(bf16[8,6144]{1,0:T(8,128)(2,1)S(1)} %bitcast.18, bf16[256,6144]{1,0:T(8,128)(2,1)S(1)} %bitcast.17, f32[8,64]{1,0:T(8,128)S(1)} %get-tuple-element.23.slab_ref), custom_call_target="tpu_custom_call" | custom-call | flops 25165824 | bytes 3500000 | tf_op jit(solution)/shard_map/back/pallas_call | solution.py:244
  89.8 3.3 %all-to-all-start.4 = ((f32[8,1,128]{2,1,0:T(1,128)}), f32[8,1,128]{2,1,0:T(1,128)S(1)}, u32[]{:S(2)}, u32[]{:S(2)}) async-start(f32[8,1,128]{2,1,0:T(1,128)} %bitcast.7), calls=%async_computation.4 | async-start | bytes 8192 | tf_op jit(solution)/shard_map/all_to_all | solution.py:349
  93.1 3.1 %project.1 = f32[32,8,256]{2,1,0:T(8,128)} custom-call(bf16[8,6144]{1,0:T(8,128)(2,1)} %bitcast.19, bf16[1536,256]{1,0:T(8,128)(2,1)} %convert_element_type.3.b0, bf16[1536,256]{1,0:T(8,128)(2,1)} %collective-permute-done.b1, bf16[1536,256]{1,0:T(8,128)(2,1)} %collective-permute-done.1.b2, bf16[1536,256]{1,0:T(8,128)(2,1)} %collective-permute-done.2.b3), custom_call_target="tpu_custom_call" | custom-call | flops 25165824 | bytes 3500000 | tf_op jit(solution)/shard_map/project/pallas_call | solution.py:213
  96.2 3.2 %all-to-all-done.4 = f32[8,1,128]{2,1,0:T(1,128)S(1)} async-done(((f32[8,1,128]{2,1,0:T(1,128)}), f32[8,1,128]{2,1,0:T(1,128)S(1)}, u32[]{:S(2)}, u32[]{:S(2)}) %all-to-all-start.4) | async-done | bytes 4128 | tf_op jit(solution)/shard_map/all_to_all | solution.py:349
  99.5 6.7 %all-to-all-start.3 = ((f32[32,8,256]{2,1,0:T(8,128)}), f32[32,8,256]{2,1,0:T(8,128)S(1)}, u32[]{:S(2)}, u32[]{:S(2)}) async-start(f32[32,8,256]{2,1,0:T(8,128)} %project.1), calls=%async_computation.3 | async-start | bytes 524288 | tf_op jit(solution)/shard_map/all_to_all | solution.py:349
  106.2 0.5 reduce_sum.11
  106.8 8.3 %all-to-all-done.3 = f32[32,8,256]{2,1,0:T(8,128)S(1)} async-done(((f32[32,8,256]{2,1,0:T(8,128)}), f32[32,8,256]{2,1,0:T(8,128)S(1)}, u32[]{:S(2)}, u32[]{:S(2)}) %all-to-all-start.3) | async-done | bytes 262176 | tf_op jit(solution)/shard_map/all_to_all | solution.py:349
  115.1 0.7 copy-done.4
  115.8 6.8 %update.1 = (bf16[384,6144]{1,0:T(8,128)(2,1)}, f32[384,256]{1,0:T(8,128)}, f32[384,256]{1,0:T(8,128)}) custom-call(bf16[384,256]{1,0:T(8,128)(2,1)} %get-tuple-element.14.codes_hbm, f32[256,256]{1,0:T(8,128)} %bitcast.28, f32[384,256]{1,0:T(8,128)} %first_ref.1, f32[384,256]{1,0:T(8,128)} %second_ref.1, bf16[1536,256]{1,0:T(8,128)(2,1)} %convert_element_type.3.b0, ...), custom_call_target="tpu_custom_call" | custom-call | flops 2415919104 | bytes 11000000 | tf_op jit(solution)/shard_map/update/pallas_call | solution.py:320
  (12 shorter events, 0.1 us)
Async XLA Ops:
  6.2 11.4 %copy-start.5 = (bf16[1,6144]{1,0:T(2,128)(2,1)S(1)}, bf16[1,6144]{1,0:T(2,128)(2,1)}, u32[]{:S(2)}) copy-start(bf16[1,6144]{1,0:T(2,128)(2,1)} %param.10) | copy-start | bytes 36868
  6.2 53.6 %copy-start.1 = (s32[256,64]{0,1:T(8,128)S(1)}, s32[256,64]{0,1:T(8,128)}, u32[]{:S(2)}) copy-start(s32[256,64]{0,1:T(8,128)} %param.9) | copy-start | bytes 196612
  6.2 53.6 %copy-start.2 = (bf16[256,64]{0,1:T(8,128)(2,1)S(1)}, bf16[256,64]{0,1:T(8,128)(2,1)}, u32[]{:S(2)}) copy-start(bf16[256,64]{0,1:T(8,128)(2,1)} %param.8) | copy-start | bytes 98308
  6.2 48.5 %all-to-all-start = ((bf16[32,8,6144]{2,1,0:T(8,128)(2,1)}), bf16[32,8,6144]{2,1,0:T(8,128)(2,1)S(1)}, u32[]{:S(2)}, u32[]{:S(2)}) async-start(bf16[32,8,6144]{2,1,0:T(8,128)(2,1)} %bitcast.26), calls=%async_computation | async-start | bytes 6291456 | tf_op jit(solution)/shard_map/all_to_all | solution.py:349
  15.0 62.7 %copy-start.3 = (f32[6144]{0:T(1024)S(1)}, f32[6144]{0:T(1024)}, u32[]{:S(2)}) copy-start(f32[6144]{0:T(1024)} %param.12) | copy-start | bytes 73732
  17.4 75.7 %collective-permute-start = (bf16[1536,256]{1,0:T(8,128)(2,1)}, bf16[1536,256]{1,0:T(8,128)(2,1)}, u32[]{:S(2)}, u32[]{:S(2)}) collective-permute-start(bf16[1536,256]{1,0:T(8,128)(2,1)} %convert_element_type.3.b0), channel_id=1, source_target_pairs={{0,1},{1,0},{2,3},{3,2},{4,5},{5,4},{6,7},{7,6},{8,9},{9,8},{10,11... | collective-permute-start | bytes 2359304 | tf_op jit(solution)/shard_map/ppermute | solution.py:363
  54.8 38.3 %collective-permute-start.2 = (bf16[1536,256]{1,0:T(8,128)(2,1)}, bf16[1536,256]{1,0:T(8,128)(2,1)}, u32[]{:S(2)}, u32[]{:S(2)}) collective-permute-start(bf16[1536,256]{1,0:T(8,128)(2,1)} %convert_element_type.3.b0), channel_id=1, source_target_pairs={{2,1},{35,0},{32,3},{1,2},{34,33},{3,32},{0,35},{33,34},{6,5},{39,... | collective-permute-start | bytes 2359304 | tf_op jit(solution)/shard_map/ppermute | solution.py:368
  56.4 36.7 %collective-permute-start.1 = (bf16[1536,256]{1,0:T(8,128)(2,1)}, bf16[1536,256]{1,0:T(8,128)(2,1)}, u32[]{:S(2)}, u32[]{:S(2)}) collective-permute-start(bf16[1536,256]{1,0:T(8,128)(2,1)} %convert_element_type.3.b0), channel_id=1, source_target_pairs={{34,0},{3,1},{0,2},{33,3},{2,32},{35,33},{32,34},{1,35},{38,4},{7,... | collective-permute-start | bytes 2359304 | tf_op jit(solution)/shard_map/ppermute | solution.py:367
  87.8 5.3 %copy-start = (bf16[1,8,48,128]{3,1,2,0:T(8,128)(2,1)}, bf16[1,8,48,128]{3,1,2,0:T(8,128)(2,1)S(1)}, u32[]{:S(2)}) copy-start(bf16[1,8,48,128]{3,1,2,0:T(8,128)(2,1)S(1)} %copy.15) | copy-start | bytes 294916
  89.8 9.7 %all-to-all-start.4 = ((f32[8,1,128]{2,1,0:T(1,128)}), f32[8,1,128]{2,1,0:T(1,128)S(1)}, u32[]{:S(2)}, u32[]{:S(2)}) async-start(f32[8,1,128]{2,1,0:T(1,128)} %bitcast.7), calls=%async_computation.4 | async-start | bytes 8192 | tf_op jit(solution)/shard_map/all_to_all | solution.py:349
  99.5 15.6 %all-to-all-start.3 = ((f32[32,8,256]{2,1,0:T(8,128)}), f32[32,8,256]{2,1,0:T(8,128)S(1)}, u32[]{:S(2)}, u32[]{:S(2)}) async-start(f32[32,8,256]{2,1,0:T(8,128)} %project.1), calls=%async_computation.3 | async-start | bytes 524288 | tf_op jit(solution)/shard_map/all_to_all | solution.py:349
  115.1 0.7 copy-start.4

commit v4 on v3

--- a/solution.py
+++ b/solution.py
@@ -128,7 +128,7 @@
     )(idx_t, val_t, weight)
 
 
-def recon_kernel(idx_ref, val_ref, recv_ref, part_ref, slab_ref):
+def select_kernel(idx_ref, val_ref, weight_ref, slab_ref):
     y_x, z, block = where_am_i()
     token = y_x * 32 + iota((8, TOK), 0) * 4 + block
     pick = jnp.where(iota((8, TOK), 1) == token, 1.0, 0.0).astype(BF)
@@ -140,7 +140,28 @@
     weight = jnp.zeros((8, TOK), F32)
     for k in range(TOPK):
         weight += jnp.where(slab[:, k : k + 1] == source, value[:, k : k + 1], 0.0)
-    weight = jnp.where((lane & 7) == iota((8, TOK), 0), weight, 0.0).astype(BF)
+    weight_ref[...] = jnp.where((lane & 7) == iota((8, TOK), 0), weight, 0.0).astype(BF)
+
+
+def select(idx_t, val_t):
+    return pl.pallas_call(
+        select_kernel,
+        in_specs=whole(2),
+        out_specs=whole(2),
+        out_shape=[
+            jax.ShapeDtypeStruct((8, TOK), BF),
+            jax.ShapeDtypeStruct((8, TOPK), F32),
+        ],
+        cost_estimate=pl.CostEstimate(
+            flops=20_000_000, bytes_accessed=200_000, transcendentals=0
+        ),
+        compiler_params=pltpu.CompilerParams(vmem_limit_bytes=10 * 1024 * 1024),
+        name="select",
+    )(idx_t, val_t)
+
+
+def recon_kernel(weight_ref, recv_ref, part_ref):
+    weight = weight_ref[...]
     step = 1024
     for j in range(MODEL // step):
         part = jnp.dot(
@@ -150,21 +171,18 @@
             part_ref[:, j * (step // 128) + c, :] = part[:, c * 128 : (c + 1) * 128]
 
 
-def partial_recon(idx_t, val_t, recv):
+def partial_recon(weight, recv):
     return pl.pallas_call(
         recon_kernel,
-        in_specs=whole(3),
-        out_specs=whole(2),
-        out_shape=[
-            jax.ShapeDtypeStruct((8, MODEL // 128, 128), F32),
-            jax.ShapeDtypeStruct((8, TOPK), F32),
-        ],
+        in_specs=whole(2),
+        out_specs=whole(1)[0],
+        out_shape=jax.ShapeDtypeStruct((8, MODEL // 128, 128), F32),
         cost_estimate=pl.CostEstimate(
             flops=2 * TOK * 8 * MODEL, bytes_accessed=4_000_000, transcendentals=0
         ),
         compiler_params=pltpu.CompilerParams(vmem_limit_bytes=10 * 1024 * 1024),
         name="partial_recon",
-    )(idx_t, val_t, recv)
+    )(weight, recv)
 
 
 def resid_kernel(part_ref, bias_ref, target_ref, resid_ref):
@@ -361,7 +379,8 @@
     recv = exchange(sent.reshape(32, 8, MODEL), PLANE).reshape(TOK, MODEL)
     own = basis.astype(BF)
     own_sib = lax.ppermute(own, "core", swap)
-    part, slab = partial_recon(idx_t, val_t, recv)
+    weight, slab = select(idx_t, val_t)
+    part = partial_recon(weight, recv)
     target = target.reshape(rows, 128)
     late, recv, target = lax.optimization_barrier((own, recv, target))
     other = lax.ppermute(late, RING, straight)

time: 123 us -> 123 us (level)
  no operation moved by 1% of the time
where the time goes in v4:
time: 123 us
  waiting for transfers between devices  48.7 us (40%)
  blocking collectives  27.1 us (22%)
  starting transfers between devices  24 us (20%)
  Pallas kernels  18.4 us (15%)
  other arithmetic  2.98 us (2%)
    all_to_all x3, waiting for transfers between devices, step(): lax.all_to_all(a, axes, split_axis=0, concat_axis=0, tiled=True)  48.7 us
    all_to_all x2, blocking collectives, step(): lax.all_to_all(a, axes, split_axis=0, concat_axis=0, tiled=True)  27.1 us
    all_to_all x3, starting transfers between devices, step(): lax.all_to_all(a, axes, split_axis=0, concat_axis=0, tiled=True)  18.8 us
    pallas_call x1, Pallas kernels, update(): pl.pallas_call(update_kernel, in_specs=[ANY] * 8, out_specs=[ANY] * 3, ou...  6.85 us
    pallas_call x1, Pallas kernels, pack(): pl.pallas_call(pack_kernel, in_specs=[ANY] * 3, out_specs=[ANY] * 2, out_...  5.56 us
    ppermute x1, starting transfers between devices, step(): other = lax.ppermute(late, RING, straight)  3.33 us
    pallas_call x1, Pallas kernels, project(): pl.pallas_call(project_kernel, in_specs=whole(5), out_specs=whole(1)[0],...  3.12 us
  transfers between devices with their start and end apart: 6, of which 3 were waited for; matrix products, arithmetic and copies ran while one was open for 2% of the time, Pallas kernels for 5%

profile of v4, /device:TPU:1, one launch (start us, length us, event | category | flops | bytes accessed | tf_op | source)
XLA Modules:
  0.0 122.7 jit_solution(7175193389054122575)
XLA Ops:
  0.6 5.6 %pack.1 = (bf16[256,6144]{1,0:T(8,128)(2,1)}, bf16[384,256]{1,0:T(8,128)(2,1)}) custom-call(s32[64,256]{1,0:T(8,128)} %bitcast.20, bf16[64,256]{1,0:T(8,128)(2,1)} %bitcast.22, bf16[384,6144]{1,0:T(8,128)(2,1)} %weight_ref.1), custom_call_target="tpu_custom_call" | custom-call | flops 1207959552 | bytes 8000000 | tf_op jit(solution)/shard_map/pack/pallas_call | solution.py:106
  6.2 0.0 copy-start.5
  6.2 0.0 copy-start.2
  6.2 8.7 %all-to-all-start = ((bf16[32,8,6144]{2,1,0:T(8,128)(2,1)}), bf16[32,8,6144]{2,1,0:T(8,128)(2,1)S(1)}, u32[]{:S(2)}, u32[]{:S(2)}) async-start(bf16[32,8,6144]{2,1,0:T(8,128)(2,1)} %bitcast.26), calls=%async_computation | async-start | bytes 6291456 | tf_op jit(solution)/shard_map/all_to_all | solution.py:367
  15.0 0.0 copy-start.3
  15.0 2.4 %convert_element_type.3.b0 = bf16[1536,256]{1,0:T(8,128)(2,1)} convert(f32[1536,256]{1,0:T(8,128)} %param.13) | non-fusion elementwise | flops 393216 | bytes 2359296 | tf_op jit(solution)/shard_map/convert_element_type | solution.py:380
  17.4 0.2 collective-permute-start
  17.6 0.1 reduce.1
  17.7 37.1 %all-to-all-done = bf16[32,8,6144]{2,1,0:T(8,128)(2,1)S(1)} async-done(((bf16[32,8,6144]{2,1,0:T(8,128)(2,1)}), bf16[32,8,6144]{2,1,0:T(8,128)(2,1)S(1)}, u32[]{:S(2)}, u32[]{:S(2)}) %all-to-all-start) | async-done | bytes 3145760 | tf_op jit(solution)/shard_map/all_to_all | solution.py:367
  54.8 1.7 %collective-permute-start.2 = (bf16[1536,256]{1,0:T(8,128)(2,1)}, bf16[1536,256]{1,0:T(8,128)(2,1)}, u32[]{:S(2)}, u32[]{:S(2)}) collective-permute-start(bf16[1536,256]{1,0:T(8,128)(2,1)} %convert_element_type.3.b0), channel_id=1, source_target_pairs={{2,1},{35,0},{32,3},{1,2},{34,33},{3,32},{0,35},{33,34},{6,5},{39,... | collective-permute-start | bytes 2359304 | tf_op jit(solution)/shard_map/ppermute | solution.py:387
  56.4 3.3 %collective-permute-start.1 = (bf16[1536,256]{1,0:T(8,128)(2,1)}, bf16[1536,256]{1,0:T(8,128)(2,1)}, u32[]{:S(2)}, u32[]{:S(2)}) collective-permute-start(bf16[1536,256]{1,0:T(8,128)(2,1)} %convert_element_type.3.b0), channel_id=1, source_target_pairs={{34,0},{3,1},{0,2},{33,3},{2,32},{35,33},{32,34},{1,35},{38,4},{7,... | collective-permute-start | bytes 2359304 | tf_op jit(solution)/shard_map/ppermute | solution.py:386
  59.8 0.4 select.1
  60.2 0.5 partial_recon.1
  60.7 16.9 %all_to_all.25.part_ref = f32[8,48,128]{2,1,0:T(8,128)S(1)} all-to-all(f32[8,48,128]{2,1,0:T(8,128)S(1)} %partial_recon.1), channel_id=1, replica_groups=mesh['y'=4,'x_hi'=2,'z'=8,'x_lo'=2,'core'=2] {'z'}, dimensions={0} | all-to-all | bytes 393216 | tf_op jit(solution)/shard_map/all_to_all | solution.py:367
  77.7 10.2 %all_to_all.26 = bf16[8,48,128]{2,1,0:T(8,128)(2,1)S(1)} all-to-all(bf16[8,48,128]{2,1,0:T(8,128)(2,1)S(1)} %residual.1), channel_id=1, replica_groups=mesh['y'=4,'x_hi'=2,'z'=8,'x_lo'=2,'core'=2] {'z'}, dimensions={0} | all-to-all | bytes 196608 | tf_op jit(solution)/shard_map/all_to_all | solution.py:367
  87.9 1.9 %back.1 = f32[8,128]{1,0:T(8,128)} custom-call(bf16[8,6144]{1,0:T(8,128)(2,1)S(1)} %bitcast.18, bf16[256,6144]{1,0:T(8,128)(2,1)S(1)} %bitcast.17, f32[8,64]{1,0:T(8,128)S(1)} %get-tuple-element.23.slab_ref), custom_call_target="tpu_custom_call" | custom-call | flops 25165824 | bytes 3500000 | tf_op jit(solution)/shard_map/back/pallas_call | solution.py:262
  89.8 3.3 %all-to-all-start.4 = ((f32[8,1,128]{2,1,0:T(1,128)}), f32[8,1,128]{2,1,0:T(1,128)S(1)}, u32[]{:S(2)}, u32[]{:S(2)}) async-start(f32[8,1,128]{2,1,0:T(1,128)} %bitcast.7), calls=%async_computation.4 | async-start | bytes 8192 | tf_op jit(solution)/shard_map/all_to_all | solution.py:367
  93.2 3.1 %project.1 = f32[32,8,256]{2,1,0:T(8,128)} custom-call(bf16[8,6144]{1,0:T(8,128)(2,1)} %bitcast.19, bf16[1536,256]{1,0:T(8,128)(2,1)} %convert_element_type.3.b0, bf16[1536,256]{1,0:T(8,128)(2,1)} %collective-permute-done.b1, bf16[1536,256]{1,0:T(8,128)(2,1)} %collective-permute-done.1.b2, bf16[1536,256]{1,0:T(8,128)(2,1)} %collective-permute-done.2.b3), custom_call_target="tpu_custom_call" | custom-call | flops 25165824 | bytes 3500000 | tf_op jit(solution)/shard_map/project/pallas_call | solution.py:231
  96.3 3.2 %all-to-all-done.4 = f32[8,1,128]{2,1,0:T(1,128)S(1)} async-done(((f32[8,1,128]{2,1,0:T(1,128)}), f32[8,1,128]{2,1,0:T(1,128)S(1)}, u32[]{:S(2)}, u32[]{:S(2)}) %all-to-all-start.4) | async-done | bytes 4128 | tf_op jit(solution)/shard_map/all_to_all | solution.py:367
  99.5 6.7 %all-to-all-start.3 = ((f32[32,8,256]{2,1,0:T(8,128)}), f32[32,8,256]{2,1,0:T(8,128)S(1)}, u32[]{:S(2)}, u32[]{:S(2)}) async-start(f32[32,8,256]{2,1,0:T(8,128)} %project.1), calls=%async_computation.3 | async-start | bytes 524288 | tf_op jit(solution)/shard_map/all_to_all | solution.py:367
  106.2 0.5 reduce_sum.11
  106.8 8.3 %all-to-all-done.3 = f32[32,8,256]{2,1,0:T(8,128)S(1)} async-done(((f32[32,8,256]{2,1,0:T(8,128)}), f32[32,8,256]{2,1,0:T(8,128)S(1)}, u32[]{:S(2)}, u32[]{:S(2)}) %all-to-all-start.3) | async-done | bytes 262176 | tf_op jit(solution)/shard_map/all_to_all | solution.py:367
  115.1 0.7 copy-done.4
  115.8 6.8 %update.1 = (bf16[384,6144]{1,0:T(8,128)(2,1)}, f32[384,256]{1,0:T(8,128)}, f32[384,256]{1,0:T(8,128)}) custom-call(bf16[384,256]{1,0:T(8,128)(2,1)} %get-tuple-element.14.codes_hbm, f32[256,256]{1,0:T(8,128)} %bitcast.28, f32[384,256]{1,0:T(8,128)} %first_ref.1, f32[384,256]{1,0:T(8,128)} %second_ref.1, bf16[1536,256]{1,0:T(8,128)(2,1)} %convert_element_type.3.b0, ...), custom_call_target="tpu_custom_call" | custom-call | flops 2415919104 | bytes 11000000 | tf_op jit(solution)/shard_map/update/pallas_call | solution.py:338
  (13 shorter events, 0.1 us)
Async XLA Ops:
  6.2 11.4 %copy-start.5 = (bf16[1,6144]{1,0:T(2,128)(2,1)S(1)}, bf16[1,6144]{1,0:T(2,128)(2,1)}, u32[]{:S(2)}) copy-start(bf16[1,6144]{1,0:T(2,128)(2,1)} %param.10) | copy-start | bytes 36868
  6.2 53.6 %copy-start.1 = (s32[256,64]{0,1:T(8,128)S(1)}, s32[256,64]{0,1:T(8,128)}, u32[]{:S(2)}) copy-start(s32[256,64]{0,1:T(8,128)} %param.9) | copy-start | bytes 196612
  6.2 53.6 %copy-start.2 = (bf16[256,64]{0,1:T(8,128)(2,1)S(1)}, bf16[256,64]{0,1:T(8,128)(2,1)}, u32[]{:S(2)}) copy-start(bf16[256,64]{0,1:T(8,128)(2,1)} %param.8) | copy-start | bytes 98308
  6.2 48.5 %all-to-all-start = ((bf16[32,8,6144]{2,1,0:T(8,128)(2,1)}), bf16[32,8,6144]{2,1,0:T(8,128)(2,1)S(1)}, u32[]{:S(2)}, u32[]{:S(2)}) async-start(bf16[32,8,6144]{2,1,0:T(8,128)(2,1)} %bitcast.26), calls=%async_computation | async-start | bytes 6291456 | tf_op jit(solution)/shard_map/all_to_all | solution.py:367
  15.0 62.7 %copy-start.3 = (f32[6144]{0:T(1024)S(1)}, f32[6144]{0:T(1024)}, u32[]{:S(2)}) copy-start(f32[6144]{0:T(1024)} %param.12) | copy-start | bytes 73732
  17.4 75.8 %collective-permute-start = (bf16[1536,256]{1,0:T(8,128)(2,1)}, bf16[1536,256]{1,0:T(8,128)(2,1)}, u32[]{:S(2)}, u32[]{:S(2)}) collective-permute-start(bf16[1536,256]{1,0:T(8,128)(2,1)} %convert_element_type.3.b0), channel_id=1, source_target_pairs={{0,1},{1,0},{2,3},{3,2},{4,5},{5,4},{6,7},{7,6},{8,9},{9,8},{10,11... | collective-permute-start | bytes 2359304 | tf_op jit(solution)/shard_map/ppermute | solution.py:381
  54.8 38.4 %collective-permute-start.2 = (bf16[1536,256]{1,0:T(8,128)(2,1)}, bf16[1536,256]{1,0:T(8,128)(2,1)}, u32[]{:S(2)}, u32[]{:S(2)}) collective-permute-start(bf16[1536,256]{1,0:T(8,128)(2,1)} %convert_element_type.3.b0), channel_id=1, source_target_pairs={{2,1},{35,0},{32,3},{1,2},{34,33},{3,32},{0,35},{33,34},{6,5},{39,... | collective-permute-start | bytes 2359304 | tf_op jit(solution)/shard_map/ppermute | solution.py:387
  56.4 36.7 %collective-permute-start.1 = (bf16[1536,256]{1,0:T(8,128)(2,1)}, bf16[1536,256]{1,0:T(8,128)(2,1)}, u32[]{:S(2)}, u32[]{:S(2)}) collective-permute-start(bf16[1536,256]{1,0:T(8,128)(2,1)} %convert_element_type.3.b0), channel_id=1, source_target_pairs={{34,0},{3,1},{0,2},{33,3},{2,32},{35,33},{32,34},{1,35},{38,4},{7,... | collective-permute-start | bytes 2359304 | tf_op jit(solution)/shard_map/ppermute | solution.py:386
  87.9 5.3 %copy-start = (bf16[1,8,48,128]{3,1,2,0:T(8,128)(2,1)}, bf16[1,8,48,128]{3,1,2,0:T(8,128)(2,1)S(1)}, u32[]{:S(2)}) copy-start(bf16[1,8,48,128]{3,1,2,0:T(8,128)(2,1)S(1)} %copy.15) | copy-start | bytes 294916
  89.8 9.7 %all-to-all-start.4 = ((f32[8,1,128]{2,1,0:T(1,128)}), f32[8,1,128]{2,1,0:T(1,128)S(1)}, u32[]{:S(2)}, u32[]{:S(2)}) async-start(f32[8,1,128]{2,1,0:T(1,128)} %bitcast.7), calls=%async_computation.4 | async-start | bytes 8192 | tf_op jit(solution)/shard_map/all_to_all | solution.py:367
  99.5 15.6 %all-to-all-start.3 = ((f32[32,8,256]{2,1,0:T(8,128)}), f32[32,8,256]{2,1,0:T(8,128)S(1)}, u32[]{:S(2)}, u32[]{:S(2)}) async-start(f32[32,8,256]{2,1,0:T(8,128)} %project.1), calls=%async_computation.3 | async-start | bytes 524288 | tf_op jit(solution)/shard_map/all_to_all | solution.py:367
  115.1 0.7 copy-start.4
